TPU v7x, 32 devices: a whole 2x2x4 slice. The times are simulated.
32 devices in a mesh: section: 4 (over y, x), dp: 8 (over z, core).
Axes of the slice: x: 2, y: 2, z: 4, core: 2. Of those that a mesh axis runs over, the one named last changes fastest.
Arguments:
- inputs: bfloat16 [4, 2, 512, 4096], P('section', None, 'dp'), may hold values from -6 to 6
- cotangent: bfloat16 [2, 512, 4096], P(None, 'dp'), may hold values from -6 to 6
- norm_gain: bfloat16 [4, 4096], P('section', 'dp'), may hold values from 0.5 to 1.5
- key_weight: bfloat16 [4, 4096, 512], P('section', 'dp'), may hold values from -0.09375 to 0.09375
- value_weight: bfloat16 [4, 4096, 512], P('section', 'dp'), may hold values from -0.09375 to 0.09375
- plan: int32 [4, 2], P('section'), may hold values from 0 to 1, each once within a row
Outputs:
- grad_inputs: bfloat16 [4, 2, 512, 4096], P('section', None, 'dp')
- key_weight_grad: float32 [4, 4096, 512], P('section', 'dp')
- value_weight_grad: float32 [4, 4096, 512], P('section', 'dp')
- gain_grad: float32 [4, 4096], P('section', 'dp')
Inputs may be any that keep to these rules, and one draw needn't show every extreme that they name: Each row of plan lists every micro-batch once.
All inputs are finite; a program needn't handle non-finite values.
Results may differ from a plain program's by a relative error of at most 0.03.
Values may be sent and summed in bfloat16 or wider, within the bound.
A program may use at most 128 MiB of HBM per device.

v0:
```python
import functools
import math

import jax
import jax.numpy as jnp
import numpy as np
from jax import lax
from jax.experimental import pallas as pl
from jax.experimental.pallas import tpu as pltpu
from jax.sharding import PartitionSpec as P

HEAD_DIM = 128
EPS = 1e-05
ROPE_BASE = 500000.0
PIECES = 4
HELPED = 1
MESH = pl.DeviceIdType.MESH
F32 = jnp.float32
BF16 = jnp.bfloat16


def dot_nn(a, b):
    return lax.dot_general(a, b, (((1,), (0,)), ((), ())), preferred_element_type=F32)


def dot_nt(a, b):
    return lax.dot_general(a, b, (((1,), (1,)), ((), ())), preferred_element_type=F32)


def dot_tn(a, b):
    return lax.dot_general(a, b, (((0,), (0,)), ((), ())), preferred_element_type=F32)


def rope_tables(length):
    half = HEAD_DIM // 2
    freq = (ROPE_BASE ** (-(np.arange(half, dtype=np.float32) * 2.0 / HEAD_DIM))).astype(np.float32)
    angles = np.arange(length, dtype=np.float32)[:, None] * freq[None, :]
    cos, sin = np.cos(angles), np.sin(angles)
    return (
        np.concatenate([cos, cos], -1).astype(np.float32),
        np.concatenate([-sin, sin], -1).astype(np.float32),
    )


def kernel(S, N, x_ref, cot_ref, gain_ref, wk_ref, wv_ref, cos_ref, sin_ref,
           low_out, gk_out, gv_out, gg_out,
           wall, ns, nall, gall, inv_s, acc, key_s, val_s, qst, prob, ubuf, lowb, gnb,
           kball, gsh, gsall, stage,
           loc, ws, wr, hs, hr, ps, pr_sem, token, rls, rlr, gsem, nsem, ssem, us, ur, uloc, kbs, kbr, krs, krr):
    B, KH, L = ubuf.shape[0], ubuf.shape[1], ubuf.shape[2]
    CW = ubuf.shape[3]
    w = wall.shape[1]
    KV = KH * HEAD_DIM
    G = CW // HEAD_DIM
    D = x_ref.shape[1]
    C = N // 2
    scale = 1.0 / math.sqrt(HEAD_DIM)
    sec = lax.axis_index("section")
    me = lax.axis_index("dp")
    c = me // 2
    core = me % 2
    partner = c * 2 + (1 - core)
    hp = w // PIECES
    OWN = PIECES - HELPED if S % 2 == 0 else PIECES
    upper = sec >= S // 2
    pair = jnp.where(upper, sec - S // 2, sec + S // 2) if S % 2 == 0 else sec

    def remote(src, dst, send, recv, peer):
        return pltpu.make_async_remote_copy(
            src_ref=src, dst_ref=dst, send_sem=send, recv_sem=recv,
            device_id=(sec, peer), device_id_type=MESH)

    def wait_all(ref, sem):
        pltpu.make_async_copy(ref, ref, sem).wait()

    ck = pltpu.make_async_copy(wk_ref, wall.at[me, :, pl.ds(0, KV)], loc.at[0])
    cv = pltpu.make_async_copy(wv_ref, wall.at[me, :, pl.ds(KV, KV)], loc.at[1])
    ck.start()
    cv.start()

    barrier = pltpu.get_barrier_semaphore()
    for i in range(1, N):
        pl.semaphore_signal(barrier, inc=1, device_id=(sec, (me + i) % N), device_id_type=MESH)

    @pl.when(sec > 0)
    def _():
        pl.semaphore_signal(barrier, inc=1, device_id=(sec - 1, me), device_id_type=MESH)

    @pl.when(sec < S - 1)
    def _():
        pl.semaphore_signal(barrier, inc=1, device_id=(sec + 1, me), device_id_type=MESH)
    helps = S % 2 == 0 and S > 2
    if helps:
        pl.semaphore_signal(barrier, inc=1, device_id=(pair, me), device_id_type=MESH)
    below = jnp.where(sec > 0, 1, 0)
    above = jnp.where(sec < S - 1, 1, 0)
    pl.semaphore_wait(barrier, N - 1 + below + above + (1 if helps else 0))

    gcopies = []
    for i in range(1, N):
        cp = remote(gain_ref, gall.at[me], gsem.at[0], gsem.at[1], (me + i) % N)
        cp.start()
        gcopies.append(cp)
    gall[me] = gain_ref[...]
    ck.wait()
    cv.wait()

    def piece(shard, p):
        return wall.at[shard, pl.ds(p * hp, hp)]

    def wcopy(way, t, p):
        chip = c - t if way == 0 else c + t
        peer = (c + 1 if way == 0 else c - 1) * 2 + core
        ref = piece(chip * 2 + core, p)
        return remote(ref, ref, ws.at[way, t, p], wr.at[way, t, p], peer)

    def wrecv(way, t, p):
        chip = c - 1 - t if way == 0 else c + 1 + t
        ref = piece(chip * 2 + core, p)
        return remote(ref, ref, ws.at[way, t, p], wr.at[way, t, p], partner)

    def relay(slot, chip, p, mine):
        ref = piece(chip * 2 + (core if mine else 1 - core), p)
        return remote(ref, ref, rls.at[slot], rlr.at[slot], partner)

    def relayed(slot, chip, mine, sem):
        wait_all(wall.at[chip * 2 + (core if mine else 1 - core)], sem.at[slot])

    def to_pair(p):
        return pltpu.make_async_remote_copy(
            src_ref=piece(me, p), dst_ref=stage.at[c, p - OWN], send_sem=ps.at[0, p - OWN],
            recv_sem=pr_sem.at[0, p - OWN], device_id=(pair, me), device_id_type=MESH)

    def hcopy(way, t, p, receive=False):
        if receive:
            chip, peer = (c - 1 - t if way == 0 else c + 1 + t), partner
        else:
            chip = c - t if way == 0 else c + t
            peer = (c + 1 if way == 0 else c - 1) * 2 + core
        ref = stage.at[chip, p - OWN]
        return remote(ref, ref, hs.at[way, t, p - OWN], hr.at[way, t, p - OWN], peer)

    def hand(way, t, p):
        chip = c - 1 - t if way == 0 else c + 1 + t
        slot = 1 + way * (C - 1) + t
        return pltpu.make_async_remote_copy(
            src_ref=stage.at[chip, p - OWN], dst_ref=piece(chip * 2 + core, p),
            send_sem=ps.at[slot, p - OWN], recv_sem=pr_sem.at[slot, p - OWN],
            device_id=(pair, me), device_id_type=MESH)

    def can_send(way, t):
        return ((c - t >= 0) & (c + 1 < C)) if way == 0 else ((c + t < C) & (c >= 1))

    def can_recv(way, t):
        return (c - 1 - t >= 0) if way == 0 else (c + 1 + t < C)

    for p in range(OWN, PIECES):
        @pl.when(upper)
        def _(p=p):
            to_pair(p).start()
    for p in range(OWN):
        for way in range(2):
            @pl.when(can_send(way, 0) & upper)
            def _(way=way, p=p):
                wcopy(way, 0, p).start()
    for p in range(PIECES):
        relay(0, c, p, True).start()

    def cot_copy(k, j):
        return pltpu.make_async_copy(
            cot_ref.at[k, :, pl.ds(j * CW, CW)], ubuf.at[k, j], uloc.at[k, j])

    @pl.when(sec == S - 1)
    def _():
        for k in range(B):
            for j in range(KH):
                cot_copy(k, j).start()

    total = jnp.zeros((B * L, 1), F32)
    for d in range(N):
        xd = x_ref[:, d * w:(d + 1) * w].astype(F32)
        total = total + jnp.sum(xd * xd, axis=-1, keepdims=True)
    inv = lax.rsqrt(total * (1.0 / D) + EPS)
    inv_s[...] = jnp.broadcast_to(inv, inv_s.shape)
    wait_all(gall.at[pl.ds(0, N - 1)], gsem.at[1])
    for d in range(N):
        xd = x_ref[:, d * w:(d + 1) * w].astype(F32)
        ns[d] = (xd * inv * gall[d][0:1, :]).astype(BF16)
        gsh[d] = jnp.zeros(gsh.shape[1:], F32)
    nall[me] = ns[me]
    cos = cos_ref[...]
    sin = sin_ref[...]

    def queries(k, carry):
        rows = pl.ds(pl.multiple_of(k * L, L), L)
        for j in range(KH):
            for g in range(G):
                col = (j * G + g) * HEAD_DIM
                v = ns[col // w, rows, col % w:col % w + HEAD_DIM].astype(F32)
                q = v * cos + pltpu.roll(v, HEAD_DIM // 2, 1) * sin
                qst[k, j, g * L:(g + 1) * L, :] = q.astype(BF16)
        return carry
    lax.fori_loop(0, B, queries, 0)

    def forward_step(t):
        for p in range(PIECES):
            for way in range(2):
                chip = c - 1 - t if way == 0 else c + 1 + t

                @pl.when(can_recv(way, t))
                def _(way=way, p=p, chip=chip):
                    def by_line():
                        wrecv(way, t, p).wait_recv()
                        if t + 1 < C - 1:
                            @pl.when(can_send(way, t + 1))
                            def _():
                                wcopy(way, t + 1, p).start()
                    if p < OWN:
                        by_line()
                    else:
                        @pl.when(upper)
                        def _():
                            hand(way, t, p).wait_recv()

                        @pl.when(jnp.logical_not(upper))
                        def _():
                            by_line()
                    relay(1 + way * (C - 1) + t, chip, p, True).start()

    def use_step(t):
        for way in range(2):
            @pl.when(can_recv(way, t))
            def _(way=way):
                chip = c - 1 - t if way == 0 else c + 1 + t
                relayed(1 + way * (C - 1) + t, chip, False, rlr)
                acc[...] += dot_nn(ns[chip * 2], wall[chip * 2]) + dot_nn(
                    ns[chip * 2 + 1], wall[chip * 2 + 1])

    @pl.when(jnp.logical_not(upper))
    def _():
        for t in range(C - 1):
            for p in range(OWN, PIECES):
                if t == 0:
                    to_pair(p).wait_recv()
                for way in range(2):
                    if t == 0:
                        @pl.when(can_send(way, 0))
                        def _(way=way, p=p):
                            hcopy(way, 0, p).start()
            for p in range(OWN, PIECES):
                for way in range(2):
                    if p == OWN:
                        for q in range(PIECES):
                            if q != t and not (t + 1 == C - 1 and q > t):
                                continue

                            @pl.when(can_send(way, 0))
                            def _(way=way, q=q):
                                wcopy(way, 0, q).start()
            for p in range(OWN, PIECES):
                for way in range(2):
                    @pl.when(can_recv(way, t))
                    def _(way=way, p=p, t=t):
                        hcopy(way, t, p, True).wait_recv()
                        if t + 1 < C - 1:
                            @pl.when(can_send(way, t + 1))
                            def _():
                                hcopy(way, t + 1, p).start()
                        hand(way, t, p).start()

    forward_step(0)
    relayed(0, c, False, rlr)
    acc[...] = dot_nn(ns[c * 2], wall[c * 2]) + dot_nn(ns[c * 2 + 1], wall[c * 2 + 1])
    for t in range(C - 1):
        if t + 1 < C - 1:
            forward_step(t + 1)
        use_step(t)

    for i in range(1, N):
        peer = (me + i) % N
        remote(ns.at[peer], nall.at[me], nsem.at[0], nsem.at[1], peer).start()

    row_pos = lax.broadcasted_iota(jnp.int32, (L, L), 0)
    col_pos = lax.broadcasted_iota(jnp.int32, (L, L), 1)
    causal = (row_pos >= col_pos)[None]

    def attend(k, carry):
        rows = pl.ds(pl.multiple_of(k * L, L), L)
        for j in range(KH):
            kp = acc[rows, j * HEAD_DIM:(j + 1) * HEAD_DIM]
            key = (kp * cos + pltpu.roll(kp, HEAD_DIM // 2, 1) * sin).astype(BF16)
            key_s[k, j] = key
            val_s[k, j] = acc[rows, KV + j * HEAD_DIM:KV + (j + 1) * HEAD_DIM].astype(BF16)
            sc = dot_nt(qst[k, j], key) * scale
            raised = jnp.where(causal, jnp.exp(sc.reshape(G, L, L)), 0.0)
            pr = raised / jnp.sum(raised, axis=-1, keepdims=True)
            prob[k, j] = pr.reshape(G * L, L)
        return carry
    lax.fori_loop(0, B, attend, 0)

    def usend(k, j):
        return pltpu.make_async_remote_copy(
            src_ref=lowb.at[k, j], dst_ref=ubuf.at[k, j], send_sem=us.at[k, j],
            recv_sem=ur.at[k, j], device_id=(lax.max(sec - 1, 0), me), device_id_type=MESH)

    def kbcopy(k, j, i):
        peer = ((c + i) % C) * 2 + core
        ref = kball.at[me, k, j]
        return remote(ref, ref, kbs.at[k, i], kbr.at[k, i], peer)

    def kbpartner(k, j):
        ref = kball.at[me, k, j]
        return remote(ref, ref, kbs.at[k, 0], kbr.at[k, 0], partner)

    def kbrelay(k, i, mine):
        chip = (c - i + C) % C
        ref = kball.at[chip * 2 + (core if mine else 1 - core), k]
        return remote(ref, ref, krs.at[k, i], krr.at[k, i], partner)

    def sent(k):
        @pl.when(sec > 0)
        def _():
            for j in range(KH):
                usend(k, j).wait_send()

    def turn(k, carry):
        rows = pl.ds(pl.multiple_of(k * L, L), L)
        keys, values = [], []
        for j in range(KH):
            @pl.when(sec == S - 1)
            def _(j=j):
                cot_copy(k, j).wait()

            @pl.when(sec < S - 1)
            def _(j=j):
                usend(k, j).wait_recv()
            u = ubuf[k, j]
            us_ = jnp.concatenate(
                [u[:, g * HEAD_DIM:(g + 1) * HEAD_DIM] for g in range(G)], axis=0)
            key, q, pr = key_s[k, j], qst[k, j], prob[k, j]
            gp = dot_nt(us_, val_s[k, j])
            gv = dot_tn(pr.astype(BF16), us_).astype(BF16)
            rd = jnp.sum(pr * gp, axis=-1, keepdims=True)
            gs = (pr * (gp - rd) * scale).astype(BF16)
            gk = dot_tn(gs, q)
            gk = (gk * cos - pltpu.roll(gk, HEAD_DIM // 2, 1) * sin).astype(BF16)
            keys.append(gk)
            values.append(gv)
            kball[me, k, j] = jnp.concatenate([gk, gv], axis=1)
            gq = dot_nn(gs, key)
            for g in range(G):
                v = gq[g * L:(g + 1) * L]
                col = (j * G + g) * HEAD_DIM
                gnb[col // w, :, col % w:col % w + HEAD_DIM] = (
                    v * cos - pltpu.roll(v, HEAD_DIM // 2, 1) * sin)
            kbpartner(k, j).start()
            for i in range(1, C):
                kbcopy(k, j, i).start()
        @pl.when((sec == S - 1) & (k > 0))
        def _():
            sent(k - 1)
            pl.semaphore_signal(token, inc=1, device_id=(sec, partner), device_id_type=MESH)
        kbv = jnp.concatenate(keys + values, axis=1)
        part_inv = inv_s[rows, 0:1]
        proj = jnp.zeros((L, 1), F32)
        for d in range(N):
            gn = gnb[d] + dot_nt(kbv, wall[d])
            gnb[d] = gn
            gt = gn * x_ref[rows, d * w:(d + 1) * w].astype(F32) * part_inv
            proj = proj + jnp.sum(gt * gall[d][0:1, :], axis=-1, keepdims=True)
            gsh[d] += jnp.sum(gt.reshape(L // 8, 8, w), axis=0)
        proj = proj * (1.0 / D) * part_inv * part_inv
        @pl.when((sec == S - 1) & ((k > 0) | (core > 0)))
        def _():
            pl.semaphore_wait(token, 1)
        for j in range(KH):
            for e in range(N // KH):
                d = j * (N // KH) + e
                u = ubuf[k, j, :, e * w:(e + 1) * w].astype(F32)
                xd = x_ref[rows, d * w:(d + 1) * w].astype(F32)
                low = (u + part_inv * gall[d][0:1, :] * gnb[d] - xd * proj).astype(BF16)
                lowb[k, j, :, e * w:(e + 1) * w] = low
                low_out[rows, d * w:(d + 1) * w] = low

            @pl.when(sec > 0)
            def _(j=j):
                usend(k, j).start()
        return carry
    lax.fori_loop(0, B, turn, 0)

    @pl.when((sec == S - 1) & (core == 0))
    def _():
        sent(B - 1)
        pl.semaphore_signal(token, inc=1, device_id=(sec, partner), device_id_type=MESH)

    gsall[me] = gsh[me]
    for i in range(1, N):
        peer = (me + i) % N
        remote(gsh.at[peer], gsall.at[me], ssem.at[0], ssem.at[1], peer).start()
    for k in range(B):
        for i in range(1, C):
            chip = (c - i + C) % C
            wait_all(kball.at[chip * 2 + core, k], kbr.at[k, i])
            kbrelay(k, i, True).start()
    wait_all(nall.at[pl.ds(0, N - 1)], nsem.at[1])
    for k in range(B):
        wait_all(kball.at[partner, k], kbr.at[k, 0])
        for i in range(1, C):
            kbrelay(k, i, False).wait_recv()
    rows_all = nall[...].reshape(N * B * L, w)
    for j in range(KH):
        back = jnp.concatenate(
            [kball[g, k, j] for g in range(N) for k in range(B)], axis=0)
        dw = dot_tn(rows_all, back)
        gk_out[:, j * HEAD_DIM:(j + 1) * HEAD_DIM] = dw[:, :HEAD_DIM]
        gv_out[:, j * HEAD_DIM:(j + 1) * HEAD_DIM] = dw[:, HEAD_DIM:]
    wait_all(gsall.at[pl.ds(0, N - 1)], ssem.at[1])
    gg = gsall[0]
    for d in range(1, N):
        gg = gg + gsall[d]
    gg_out[...] = jnp.broadcast_to(jnp.sum(gg, axis=0, keepdims=True), gg_out.shape)

    wait_all(gall.at[pl.ds(0, N - 1)], gsem.at[0])
    wait_all(nall.at[pl.ds(0, N - 1)], nsem.at[0])
    wait_all(gsall.at[pl.ds(0, N - 1)], ssem.at[0])
    relayed(0, c, True, rls)
    for way in range(2):
        for t in range(C - 1):
            for p in range(PIECES):
                @pl.when(can_send(way, t) if p < OWN else can_send(way, t) & jnp.logical_not(upper))
                def _(way=way, t=t, p=p):
                    wcopy(way, t, p).wait_send()

            @pl.when(can_recv(way, t))
            def _(way=way, t=t):
                chip = c - 1 - t if way == 0 else c + 1 + t
                relayed(1 + way * (C - 1) + t, chip, True, rls)
            for p in range(OWN, PIECES):
                @pl.when(can_send(way, t) & jnp.logical_not(upper))
                def _(way=way, t=t, p=p):
                    hcopy(way, t, p).wait_send()

                @pl.when(can_recv(way, t) & jnp.logical_not(upper))
                def _(way=way, t=t, p=p):
                    hand(way, t, p).wait_send()
    for p in range(OWN, PIECES):
        @pl.when(upper)
        def _(p=p):
            to_pair(p).wait_send()
    for k in range(B):
        for i in range(C):
            wait_all(kball.at[me, k], kbs.at[k, i])
            if i:
                kbrelay(k, i, True).wait_send()

    @pl.when(sec < S - 1)
    def _():
        for k in range(B):
            sent(k)

    @pl.when((sec == S - 1) & (core == 1))
    def _():
        sent(B - 1)


def body(S, N, inputs, cotangent, norm_gain, key_weight, value_weight, plan):
    B, L, D = inputs.shape[1:]
    w, KV = key_weight.shape[1:]
    KH = KV // HEAD_DIM
    CW = D // KH
    G = CW // HEAD_DIM
    C = N // 2
    cos, sin = rope_tables(L)
    gain8 = jnp.broadcast_to(norm_gain.astype(F32), (8, w))
    vmem = pl.BlockSpec(memory_space=pltpu.VMEM)
    hbm = pl.BlockSpec(memory_space=pl.ANY)
    dma = pltpu.SemaphoreType.DMA
    low, gk, gv, gg = pl.pallas_call(
        functools.partial(kernel, S, N),
        out_shape=(
            jax.ShapeDtypeStruct((B * L, D), BF16),
            jax.ShapeDtypeStruct((w, KV), F32),
            jax.ShapeDtypeStruct((w, KV), F32),
            jax.ShapeDtypeStruct((8, w), F32),
        ),
        in_specs=[vmem, hbm, vmem, hbm, hbm, vmem, vmem],
        out_specs=(vmem,) * 4,
        scratch_shapes=[
            pltpu.VMEM((N, w, 2 * KV), BF16),
            pltpu.VMEM((N, B * L, w), BF16),
            pltpu.VMEM((N, B * L, w), BF16),
            pltpu.VMEM((N, 8, w), F32),
            pltpu.VMEM((B * L, 128), F32),
            pltpu.VMEM((B * L, 2 * KV), F32),
            pltpu.VMEM((B, KH, L, HEAD_DIM), BF16),
            pltpu.VMEM((B, KH, L, HEAD_DIM), BF16),
            pltpu.VMEM((B, KH, G * L, HEAD_DIM), BF16),
            pltpu.VMEM((B, KH, G * L, L), F32),
            pltpu.VMEM((B, KH, L, CW), BF16),
            pltpu.VMEM((B, KH, L, CW), BF16),
            pltpu.VMEM((N, L, w), F32),
            pltpu.VMEM((N, B, KH, L, 2 * HEAD_DIM), BF16),
            pltpu.VMEM((N, 8, w), F32),
            pltpu.VMEM((N, 8, w), F32),
            pltpu.VMEM((C, HELPED, w // PIECES, 2 * KV), BF16),
            dma((2,)),
            dma((2, C - 1, PIECES)),
            dma((2, C - 1, PIECES)),
            dma((2, C - 1, HELPED)),
            dma((2, C - 1, HELPED)),
            dma((2 * C - 1, HELPED)),
            dma((2 * C - 1, HELPED)),
            pltpu.SemaphoreType.REGULAR,
            dma((2 * C - 1,)),
            dma((2 * C - 1,)),
            dma((2,)),
            dma((2,)),
            dma((2,)),
            dma((B, KH)),
            dma((B, KH)),
            dma((B, KH)),
            dma((B, C)),
            dma((B, C)),
            dma((B, C)),
            dma((B, C)),
        ],
        compiler_params=pltpu.CompilerParams(
            collective_id=0, has_side_effects=True, vmem_limit_bytes=56 * 1024 * 1024),
    )(inputs[0].reshape(B * L, D), cotangent, gain8, key_weight[0], value_weight[0],
      jnp.asarray(cos), jnp.asarray(sin))
    low = low.reshape(B, L, D)
    selector = plan[0][:, None] == jnp.arange(B, dtype=jnp.int32)[None, :]
    ordered = jnp.sum(
        jnp.where(selector[:, :, None, None], low[None], jnp.zeros((), BF16)), axis=1)
    return ordered[None], gk[None], gv[None], gg[0:1]


def solution(mesh):
    in_specs = (
        P("section", None, "dp", None),
        P(None, "dp", None),
        P("section", "dp"),
        P("section", "dp", None),
        P("section", "dp", None),
        P("section", None),
    )
    out_specs = (
        P("section", None, "dp", None),
        P("section", "dp", None),
        P("section", "dp", None),
        P("section", "dp"),
    )
    run = functools.partial(body, mesh.shape["section"], mesh.shape["dp"])
    return jax.shard_map(run, mesh=mesh, in_specs=in_specs, out_specs=out_specs, check_vma=False)
```

profile of v0, /device:TPU:0, one launch (start us, length us, event | category | flops | bytes accessed | tf_op | source)
XLA Modules:
  0.0 165.3 jit_solution(11252064426234338238)
XLA Ops:
  0.6 0.7 iota_compare_fusion
  1.4 0.7 broadcast_in_dim.53
  2.0 0.6 broadcast_in_dim.46.gain_ref
  2.7 155.7 %shard_map.111 = (bf16[128,4096]{1,0:T(8,128)(2,1)}, f32[512,512]{1,0:T(8,128)}, f32[512,512]{1,0:T(8,128)}, f32[8,512]{1,0:T(8,128)}) custom-call(bf16[128,4096]{1,0:T(8,128)(2,1)} %bitcast.9, bf16[2,64,4096]{2,1,0:T(8,128)(2,1)} %cot_ref.1, f32[8,512]{1,0:T(8,128)} %broadcast_in_dim.46.gain_ref, bf16[512,512]{1,0:T(8,128)(2,1)} %bitcast.14, ...), custom_call_target="tpu_custom_call" | custom-call | tf_op jit(solution)/shard_map/pallas_call | solution.py:478
  158.3 0.0 copy-start.1
  158.3 3.1 %select_reduce_fusion = bf16[2,64,4096]{2,1,0:T(8,128)(2,1)} fusion(pred[2,2]{1,0:T(4,128)(4,1)S(1)} %iota_compare_fusion, bf16[2,64,4096]{2,1,0:T(8,128)(2,1)} %bitcast.11), kind=kLoop, calls=%fused_computation | loop fusion | flops 1572864 | bytes 2097156 | tf_op jit(solution)/shard_map/reduce_sum | solution.py:533
  161.4 1.3 slice.3
  162.7 0.0 copy-done.1
  162.7 0.0 copy-start
  162.7 1.0 copy.14
  163.7 0.6 copy-done
  164.3 1.0 copy.15
Async XLA Ops:
  158.3 4.4 %copy-start.1 = (f32[512,512]{1,0:T(8,128)S(1)}, f32[512,512]{1,0:T(8,128)}, u32[]{:S(2)}) copy-start(f32[512,512]{1,0:T(8,128)} %get-tuple-element.9) | copy-start | bytes 3145732
  162.7 1.6 copy-start
where the time goes:
time: 166 us; the launch traced here: 165 us
  Pallas kernels  156 us (94%)
  other arithmetic  4.5 us (3%)
  local copies, waits for them, and re-layouts  4.48 us (3%)
    pallas_call x1, Pallas kernels, body(): pl.pallas_call(functools.partial(kernel, S, N), out_shape=(jax.ShapeDtype...  156 us

commit v1 on v0

--- a/solution.py
+++ b/solution.py
@@ -12,8 +12,9 @@
 HEAD_DIM = 128
 EPS = 1e-05
 ROPE_BASE = 500000.0
-PIECES = 4
-HELPED = 1
+UNITS = 8
+DIRECT = (4, 4, 3, 3)
+ACROSS = (4, 4, 5, 3)
 MESH = pl.DeviceIdType.MESH
 F32 = jnp.float32
 BF16 = jnp.bfloat16
@@ -42,11 +43,24 @@
     )
 
 
+def shares(S):
+    if S % 4:
+        return False, (UNITS,) * 4, (0,) * 4, (0,) * 4
+    return True, DIRECT, ACROSS, tuple(UNITS - d - a for d, a in zip(DIRECT, ACROSS))
+
+
+def line_slots(S):
+    shared, direct, across, near = shares(S)
+    before = (across[2], across[3], near[3], 0)
+    after = (0, 0, across[0], across[1])
+    return max(before[r] + direct[r] + after[r] for r in range(4))
+
+
 def kernel(S, N, x_ref, cot_ref, gain_ref, wk_ref, wv_ref, cos_ref, sin_ref,
            low_out, gk_out, gv_out, gg_out,
            wall, ns, nall, gall, inv_s, acc, key_s, val_s, qst, prob, ubuf, lowb, gnb,
            kball, gsh, gsall, stage,
-           loc, ws, wr, hs, hr, ps, pr_sem, token, rls, rlr, gsem, nsem, ssem, us, ur, uloc, kbs, kbr, krs, krr):
+           loc, ws, wr, hs, hr, es, er, token, rls, rlr, gsem, nsem, ssem, us, ur, uloc, kbs, kbr, krs, krr):
     B, KH, L = ubuf.shape[0], ubuf.shape[1], ubuf.shape[2]
     CW = ubuf.shape[3]
     w = wall.shape[1]
@@ -60,10 +74,26 @@
     c = me // 2
     core = me % 2
     partner = c * 2 + (1 - core)
-    hp = w // PIECES
-    OWN = PIECES - HELPED if S % 2 == 0 else PIECES
-    upper = sec >= S // 2
-    pair = jnp.where(upper, sec - S // 2, sec + S // 2) if S % 2 == 0 else sec
+    hp = w // UNITS
+    role = sec % 4
+    shared, direct, across, near = shares(S)
+
+    def by_role(values):
+        out = jnp.int32(values[3])
+        for r in range(3):
+            out = jnp.where(role == r, jnp.int32(values[r]), out)
+        return out
+
+    up = role >= 2
+    pair = jnp.where(up, sec - 2, sec + 2) if shared else sec
+    first = (direct[2], direct[3], direct[3] + across[3], 0)
+    counts = (across[2], across[3], near[3], 0)
+    last = (0, 0, direct[0], direct[1])
+    after = (0, 0, across[0], across[1])
+    lo0, n0 = by_role(first), by_role(counts)
+    n1 = by_role(direct)
+    lo2, n2 = by_role(last), by_role(after)
+    owner0 = jnp.where(role == 2, sec + 1, pair)
 
     def remote(src, dst, send, recv, peer):
         return pltpu.make_async_remote_copy(
@@ -89,7 +119,7 @@
     @pl.when(sec < S - 1)
     def _():
         pl.semaphore_signal(barrier, inc=1, device_id=(sec + 1, me), device_id_type=MESH)
-    helps = S % 2 == 0 and S > 2
+    helps = shared
     if helps:
         pl.semaphore_signal(barrier, inc=1, device_id=(pair, me), device_id_type=MESH)
     below = jnp.where(sec > 0, 1, 0)
@@ -108,16 +138,15 @@
     def piece(shard, p):
         return wall.at[shard, pl.ds(p * hp, hp)]
 
-    def wcopy(way, t, p):
-        chip = c - t if way == 0 else c + t
+    def chip_of(way, t):
+        return c - 1 - t if way == 0 else c + 1 + t
+
+    def line_copy(way, t, v, ref):
         peer = (c + 1 if way == 0 else c - 1) * 2 + core
-        ref = piece(chip * 2 + core, p)
-        return remote(ref, ref, ws.at[way, t, p], wr.at[way, t, p], peer)
-
-    def wrecv(way, t, p):
-        chip = c - 1 - t if way == 0 else c + 1 + t
-        ref = piece(chip * 2 + core, p)
-        return remote(ref, ref, ws.at[way, t, p], wr.at[way, t, p], partner)
+        return remote(ref, ref, ws.at[way, t, v], wr.at[way, t, v], peer)
+
+    def held(help_, chip, v, p):
+        return stage.at[chip, v] if help_ else piece(chip * 2 + core, p)
 
     def relay(slot, chip, p, mine):
         ref = piece(chip * 2 + (core if mine else 1 - core), p)
@@ -126,27 +155,16 @@
     def relayed(slot, chip, mine, sem):
         wait_all(wall.at[chip * 2 + (core if mine else 1 - core)], sem.at[slot])
 
-    def to_pair(p):
+    def enter(p, v, helper):
         return pltpu.make_async_remote_copy(
-            src_ref=piece(me, p), dst_ref=stage.at[c, p - OWN], send_sem=ps.at[0, p - OWN],
-            recv_sem=pr_sem.at[0, p - OWN], device_id=(pair, me), device_id_type=MESH)
-
-    def hcopy(way, t, p, receive=False):
-        if receive:
-            chip, peer = (c - 1 - t if way == 0 else c + 1 + t), partner
-        else:
-            chip = c - t if way == 0 else c + t
-            peer = (c + 1 if way == 0 else c - 1) * 2 + core
-        ref = stage.at[chip, p - OWN]
-        return remote(ref, ref, hs.at[way, t, p - OWN], hr.at[way, t, p - OWN], peer)
-
-    def hand(way, t, p):
-        chip = c - 1 - t if way == 0 else c + 1 + t
-        slot = 1 + way * (C - 1) + t
+            src_ref=piece(me, p), dst_ref=stage.at[c, v], send_sem=es.at[p],
+            recv_sem=er.at[v], device_id=(helper, me), device_id_type=MESH)
+
+    def hand(way, t, v, p, owner):
         return pltpu.make_async_remote_copy(
-            src_ref=stage.at[chip, p - OWN], dst_ref=piece(chip * 2 + core, p),
-            send_sem=ps.at[slot, p - OWN], recv_sem=pr_sem.at[slot, p - OWN],
-            device_id=(pair, me), device_id_type=MESH)
+            src_ref=stage.at[chip_of(way, t), v], dst_ref=piece(chip_of(way, t) * 2 + core, p),
+            send_sem=hs.at[way, t, v], recv_sem=hr.at[way, t, p],
+            device_id=(owner, me), device_id_type=MESH)
 
     def can_send(way, t):
         return ((c - t >= 0) & (c + 1 < C)) if way == 0 else ((c + t < C) & (c >= 1))
@@ -154,17 +172,81 @@
     def can_recv(way, t):
         return (c - 1 - t >= 0) if way == 0 else (c + 1 + t < C)
 
-    for p in range(OWN, PIECES):
-        @pl.when(upper)
-        def _(p=p):
-            to_pair(p).start()
-    for p in range(OWN):
-        for way in range(2):
-            @pl.when(can_send(way, 0) & upper)
-            def _(way=way, p=p):
-                wcopy(way, 0, p).start()
-    for p in range(PIECES):
-        relay(0, c, p, True).start()
+    def loop(lo, n, f):
+        def step(i, carry):
+            f(lo + i, i)
+            return carry
+        lax.fori_loop(0, n, step, 0)
+
+    JOBS = ((lo0, n0, 0, True, owner0), (0, n1, n0, False, sec), (lo2, n2, n0 + n1, True, pair))
+
+    def send_own(job):
+        lo, n, base, help_, owner = JOBS[job]
+
+        def one(p, i):
+            v = base + i
+            if help_:
+                enter(p, v, owner).wait_recv()
+            for way in range(2):
+                @pl.when(can_send(way, 0))
+                def _(way=way):
+                    line_copy(way, 0, v, held(help_, c, v, p)).start()
+        loop(lo, n, one)
+
+    def serve(job, t):
+        lo, n, base, help_, owner = JOBS[job]
+
+        def one(p, i):
+            v = base + i
+            for way in range(2):
+                @pl.when(can_recv(way, t))
+                def _(way=way):
+                    chip = chip_of(way, t)
+                    ref = held(help_, chip, v, p)
+                    line_copy(way, t, v, ref).wait_recv()
+                    if t + 1 < C - 1:
+                        @pl.when(can_send(way, t + 1))
+                        def _():
+                            line_copy(way, t + 1, v, ref).start()
+                    if help_:
+                        hand(way, t, v, p, owner).start()
+                    else:
+                        relay(1 + way * (C - 1) + t, chip, p, True).start()
+        loop(lo, n, one)
+
+    def handed(t):
+        def one(p, i):
+            for way in range(2):
+                @pl.when(can_recv(way, t))
+                def _(way=way):
+                    chip = chip_of(way, t)
+                    ref = piece(chip * 2 + core, p)
+                    remote(ref, ref, hs.at[way, t, 0], hr.at[way, t, p], partner).wait_recv()
+                    relay(1 + way * (C - 1) + t, chip, p, True).start()
+        loop(n1, UNITS - n1, one)
+
+    def enter_all(act):
+        if not shared:
+            return
+        far = by_role((near[3] + direct[2], direct[3], 0, 0))
+
+        def one(p, i):
+            act(enter(p, far + i, pair))
+        loop(n1, by_role(across), one)
+
+        @pl.when(role == 3)
+        def _():
+            def other(p, i):
+                act(enter(p, i, sec - 1))
+            loop(direct[3] + across[3], near[3], other)
+
+    enter_all(lambda copy: copy.start())
+
+    @pl.when(n0 == 0)
+    def _():
+        send_own(1)
+    remote(wall.at[me], wall.at[me], rls.at[0], rlr.at[0], partner).start()
+    send_own(0)
 
     def cot_copy(k, j):
         return pltpu.make_async_copy(
@@ -202,31 +284,6 @@
         return carry
     lax.fori_loop(0, B, queries, 0)
 
-    def forward_step(t):
-        for p in range(PIECES):
-            for way in range(2):
-                chip = c - 1 - t if way == 0 else c + 1 + t
-
-                @pl.when(can_recv(way, t))
-                def _(way=way, p=p, chip=chip):
-                    def by_line():
-                        wrecv(way, t, p).wait_recv()
-                        if t + 1 < C - 1:
-                            @pl.when(can_send(way, t + 1))
-                            def _():
-                                wcopy(way, t + 1, p).start()
-                    if p < OWN:
-                        by_line()
-                    else:
-                        @pl.when(upper)
-                        def _():
-                            hand(way, t, p).wait_recv()
-
-                        @pl.when(jnp.logical_not(upper))
-                        def _():
-                            by_line()
-                    relay(1 + way * (C - 1) + t, chip, p, True).start()
-
     def use_step(t):
         for way in range(2):
             @pl.when(can_recv(way, t))
@@ -236,49 +293,35 @@
                 acc[...] += dot_nn(ns[chip * 2], wall[chip * 2]) + dot_nn(
                     ns[chip * 2 + 1], wall[chip * 2 + 1])
 
-    @pl.when(jnp.logical_not(upper))
-    def _():
-        for t in range(C - 1):
-            for p in range(OWN, PIECES):
-                if t == 0:
-                    to_pair(p).wait_recv()
-                for way in range(2):
-                    if t == 0:
-                        @pl.when(can_send(way, 0))
-                        def _(way=way, p=p):
-                            hcopy(way, 0, p).start()
-            for p in range(OWN, PIECES):
-                for way in range(2):
-                    if p == OWN:
-                        for q in range(PIECES):
-                            if q != t and not (t + 1 == C - 1 and q > t):
-                                continue
-
-                            @pl.when(can_send(way, 0))
-                            def _(way=way, q=q):
-                                wcopy(way, 0, q).start()
-            for p in range(OWN, PIECES):
-                for way in range(2):
-                    @pl.when(can_recv(way, t))
-                    def _(way=way, p=p, t=t):
-                        hcopy(way, t, p, True).wait_recv()
-                        if t + 1 < C - 1:
-                            @pl.when(can_send(way, t + 1))
-                            def _():
-                                hcopy(way, t + 1, p).start()
-                        hand(way, t, p).start()
-
-    forward_step(0)
+    def send_rows():
+        for i in range(1, N):
+            peer = (me + i) % N
+            remote(ns.at[peer], nall.at[me], nsem.at[0], nsem.at[1], peer).start()
+
+    for t in range(C - 1):
+        serve(0, t)
+        if t == 0:
+            @pl.when(n0 > 0)
+            def _():
+                send_own(1)
     relayed(0, c, False, rlr)
     acc[...] = dot_nn(ns[c * 2], wall[c * 2]) + dot_nn(ns[c * 2 + 1], wall[c * 2 + 1])
     for t in range(C - 1):
-        if t + 1 < C - 1:
-            forward_step(t + 1)
-        use_step(t)
-
-    for i in range(1, N):
-        peer = (me + i) % N
-        remote(ns.at[peer], nall.at[me], nsem.at[0], nsem.at[1], peer).start()
+        serve(1, t)
+        if t == 0:
+            send_own(2)
+        if t > 0:
+            handed(t - 1)
+        if t > 1:
+            use_step(t - 2)
+    handed(C - 2)
+    if C > 2:
+        use_step(C - 3)
+    use_step(C - 2)
+
+    @pl.when(n2 == 0)
+    def _():
+        send_rows()
 
     row_pos = lax.broadcasted_iota(jnp.int32, (L, L), 0)
     col_pos = lax.broadcasted_iota(jnp.int32, (L, L), 1)
@@ -388,6 +431,13 @@
         return carry
     lax.fori_loop(0, B, turn, 0)
 
+    for t in range(C - 1):
+        serve(2, t)
+
+    @pl.when(n2 > 0)
+    def _():
+        send_rows()
+
     @pl.when((sec == S - 1) & (core == 0))
     def _():
         sent(B - 1)
@@ -424,29 +474,26 @@
     wait_all(nall.at[pl.ds(0, N - 1)], nsem.at[0])
     wait_all(gsall.at[pl.ds(0, N - 1)], ssem.at[0])
     relayed(0, c, True, rls)
-    for way in range(2):
-        for t in range(C - 1):
-            for p in range(PIECES):
-                @pl.when(can_send(way, t) if p < OWN else can_send(way, t) & jnp.logical_not(upper))
-                def _(way=way, t=t, p=p):
-                    wcopy(way, t, p).wait_send()
-
+    enter_all(lambda copy: copy.wait_send())
+    for t in range(C - 1):
+        for job in range(3):
+            lo, n, base, help_, owner = JOBS[job]
+
+            def done(p, i, t=t, base=base, help_=help_, owner=owner):
+                v = base + i
+                for way in range(2):
+                    @pl.when(can_send(way, t))
+                    def _(way=way):
+                        line_copy(way, t, v, held(help_, c, v, p)).wait_send()
+                    if help_:
+                        @pl.when(can_recv(way, t))
+                        def _(way=way):
+                            hand(way, t, v, p, owner).wait_send()
+            loop(lo, n, done)
+        for way in range(2):
             @pl.when(can_recv(way, t))
             def _(way=way, t=t):
-                chip = c - 1 - t if way == 0 else c + 1 + t
-                relayed(1 + way * (C - 1) + t, chip, True, rls)
-            for p in range(OWN, PIECES):
-                @pl.when(can_send(way, t) & jnp.logical_not(upper))
-                def _(way=way, t=t, p=p):
-                    hcopy(way, t, p).wait_send()
-
-                @pl.when(can_recv(way, t) & jnp.logical_not(upper))
-                def _(way=way, t=t, p=p):
-                    hand(way, t, p).wait_send()
-    for p in range(OWN, PIECES):
-        @pl.when(upper)
-        def _(p=p):
-            to_pair(p).wait_send()
+                relayed(1 + way * (C - 1) + t, chip_of(way, t), True, rls)
     for k in range(B):
         for i in range(C):
             wait_all(kball.at[me, k], kbs.at[k, i])
@@ -470,6 +517,7 @@
     CW = D // KH
     G = CW // HEAD_DIM
     C = N // 2
+    slots = line_slots(S)
     cos, sin = rope_tables(L)
     gain8 = jnp.broadcast_to(norm_gain.astype(F32), (8, w))
     vmem = pl.BlockSpec(memory_space=pltpu.VMEM)
@@ -502,14 +550,14 @@
             pltpu.VMEM((N, B, KH, L, 2 * HEAD_DIM), BF16),
             pltpu.VMEM((N, 8, w), F32),
             pltpu.VMEM((N, 8, w), F32),
-            pltpu.VMEM((C, HELPED, w // PIECES, 2 * KV), BF16),
+            pltpu.VMEM((C, slots, w // UNITS, 2 * KV), BF16),
             dma((2,)),
-            dma((2, C - 1, PIECES)),
-            dma((2, C - 1, PIECES)),
-            dma((2, C - 1, HELPED)),
-            dma((2, C - 1, HELPED)),
-            dma((2 * C - 1, HELPED)),
-            dma((2 * C - 1, HELPED)),
+            dma((2, C - 1, slots)),
+            dma((2, C - 1, slots)),
+            dma((2, C - 1, slots)),
+            dma((2, C - 1, UNITS)),
+            dma((UNITS,)),
+            dma((slots,)),
             pltpu.SemaphoreType.REGULAR,
             dma((2 * C - 1,)),
             dma((2 * C - 1,)),

time: 166 us -> 191 us (1.15); the launches traced: 165 us -> 188 us
  Pallas kernels: 156 us -> 178 us
    pallas_call x1, Pallas kernels: 156 us -> 178 us  [body(): pl.pallas_call(functools.partial(kernel, S, N), out_shape=(jax.ShapeDtype...]
where the time goes in v1:
time: 191 us; the launch traced here: 188 us
  Pallas kernels  178 us (93%)
  other arithmetic  4.5 us (2%)
  local copies, waits for them, and re-layouts  4.48 us (2%)
    pallas_call x1, Pallas kernels, body(): pl.pallas_call(functools.partial(kernel, S, N), out_shape=(jax.ShapeDtype...  178 us

profile of v1, /device:TPU:0, one launch (start us, length us, event | category | flops | bytes accessed | tf_op | source)
XLA Modules:
  0.0 188.0 jit_solution(12242079711813801666)
XLA Ops:
  0.6 0.7 iota_compare_fusion
  1.4 0.7 broadcast_in_dim.53
  2.0 0.6 broadcast_in_dim.46.gain_ref
  2.7 178.4 %shard_map.111 = (bf16[128,4096]{1,0:T(8,128)(2,1)}, f32[512,512]{1,0:T(8,128)}, f32[512,512]{1,0:T(8,128)}, f32[8,512]{1,0:T(8,128)}) custom-call(bf16[128,4096]{1,0:T(8,128)(2,1)} %bitcast.9, bf16[2,64,4096]{2,1,0:T(8,128)(2,1)} %cot_ref.1, f32[8,512]{1,0:T(8,128)} %broadcast_in_dim.46.gain_ref, bf16[512,512]{1,0:T(8,128)(2,1)} %bitcast.14, ...), custom_call_target="tpu_custom_call" | custom-call | tf_op jit(solution)/shard_map/pallas_call | solution.py:526
  181.0 0.0 copy-start.1
  181.1 3.1 %select_reduce_fusion = bf16[2,64,4096]{2,1,0:T(8,128)(2,1)} fusion(pred[2,2]{1,0:T(4,128)(4,1)S(1)} %iota_compare_fusion, bf16[2,64,4096]{2,1,0:T(8,128)(2,1)} %bitcast.11), kind=kLoop, calls=%fused_computation | loop fusion | flops 1572864 | bytes 2097156 | tf_op jit(solution)/shard_map/reduce_sum | solution.py:581
  184.1 1.3 slice.3
  185.4 0.0 copy-done.1
  185.4 0.0 copy-start
  185.4 1.0 copy.14
  186.4 0.6 copy-done
  187.0 1.0 copy.15
Async XLA Ops:
  181.0 4.4 %copy-start.1 = (f32[512,512]{1,0:T(8,128)S(1)}, f32[512,512]{1,0:T(8,128)}, u32[]{:S(2)}) copy-start(f32[512,512]{1,0:T(8,128)} %get-tuple-element.9) | copy-start | bytes 3145732
  185.4 1.6 copy-start

commit v2 on v1

--- a/solution.py
+++ b/solution.py
@@ -12,9 +12,8 @@
 HEAD_DIM = 128
 EPS = 1e-05
 ROPE_BASE = 500000.0
-UNITS = 8
-DIRECT = (4, 4, 3, 3)
-ACROSS = (4, 4, 5, 3)
+DIRECT = (8, 9, 7, 6)
+ACROSS = (5, 7, 9, 5)
 MESH = pl.DeviceIdType.MESH
 F32 = jnp.float32
 BF16 = jnp.bfloat16
@@ -43,16 +42,19 @@
     )
 
 
-def shares(S):
+def shares(S, w):
+    units = 16 if w % 256 == 0 else 8
     if S % 4:
-        return False, (UNITS,) * 4, (0,) * 4, (0,) * 4
-    return True, DIRECT, ACROSS, tuple(UNITS - d - a for d, a in zip(DIRECT, ACROSS))
-
-
-def line_slots(S):
-    shared, direct, across, near = shares(S)
+        return units, False, (units,) * 4, (0,) * 4, (0,) * 4
+    direct = tuple(d * units // 16 for d in DIRECT)
+    across = tuple(a * units // 16 if r in (0, 3) else units - direct[r] for r, a in enumerate(ACROSS))
+    return units, True, direct, across, tuple(units - d - a for d, a in zip(direct, across))
+
+
+def line_slots(S, w):
+    units, shared, direct, across, near = shares(S, w)
     before = (across[2], across[3], near[3], 0)
-    after = (0, 0, across[0], across[1])
+    after = (0, 0, across[0], across[1] + near[0])
     return max(before[r] + direct[r] + after[r] for r in range(4))
 
 
@@ -60,7 +62,7 @@
            low_out, gk_out, gv_out, gg_out,
            wall, ns, nall, gall, inv_s, acc, key_s, val_s, qst, prob, ubuf, lowb, gnb,
            kball, gsh, gsall, stage,
-           loc, ws, wr, hs, hr, es, er, token, rls, rlr, gsem, nsem, ssem, us, ur, uloc, kbs, kbr, krs, krr):
+           loc, ws, wr, hs, hr, es, er, token, release, rls, rlr, gsem, nsem, ssem, us, ur, uloc, kbs, kbr, krs, krr, kfs):
     B, KH, L = ubuf.shape[0], ubuf.shape[1], ubuf.shape[2]
     CW = ubuf.shape[3]
     w = wall.shape[1]
@@ -74,9 +76,9 @@
     c = me // 2
     core = me % 2
     partner = c * 2 + (1 - core)
+    role = sec % 4
+    UNITS, shared, direct, across, near = shares(S, w)
     hp = w // UNITS
-    role = sec % 4
-    shared, direct, across, near = shares(S)
 
     def by_role(values):
         out = jnp.int32(values[3])
@@ -94,6 +96,7 @@
     n1 = by_role(direct)
     lo2, n2 = by_role(last), by_role(after)
     owner0 = jnp.where(role == 2, sec + 1, pair)
+    n3 = by_role((0, 0, 0, near[0]))
 
     def remote(src, dst, send, recv, peer):
         return pltpu.make_async_remote_copy(
@@ -119,12 +122,16 @@
     @pl.when(sec < S - 1)
     def _():
         pl.semaphore_signal(barrier, inc=1, device_id=(sec + 1, me), device_id_type=MESH)
-    helps = shared
-    if helps:
-        pl.semaphore_signal(barrier, inc=1, device_id=(pair, me), device_id_type=MESH)
+    if shared:
+        first_sec = sec - role
+        for step in range(1, 4):
+            for i in range(C):
+                pl.semaphore_signal(
+                    barrier, inc=1, device_id=(first_sec + (role + step) % 4, i * 2 + core),
+                    device_id_type=MESH)
     below = jnp.where(sec > 0, 1, 0)
     above = jnp.where(sec < S - 1, 1, 0)
-    pl.semaphore_wait(barrier, N - 1 + below + above + (1 if helps else 0))
+    pl.semaphore_wait(barrier, N - 1 + below + above + (3 * C if shared else 0))
 
     gcopies = []
     for i in range(1, N):
@@ -145,9 +152,6 @@
         peer = (c + 1 if way == 0 else c - 1) * 2 + core
         return remote(ref, ref, ws.at[way, t, v], wr.at[way, t, v], peer)
 
-    def held(help_, chip, v, p):
-        return stage.at[chip, v] if help_ else piece(chip * 2 + core, p)
-
     def relay(slot, chip, p, mine):
         ref = piece(chip * 2 + (core if mine else 1 - core), p)
         return remote(ref, ref, rls.at[slot], rlr.at[slot], partner)
@@ -160,11 +164,17 @@
             src_ref=piece(me, p), dst_ref=stage.at[c, v], send_sem=es.at[p],
             recv_sem=er.at[v], device_id=(helper, me), device_id_type=MESH)
 
-    def hand(way, t, v, p, owner):
+    def deliver(way, chip, kind, t, v, p, owner):
+        peer = (chip + t + 1 if way == 0 else chip - t - 1) * 2 + core
         return pltpu.make_async_remote_copy(
-            src_ref=stage.at[chip_of(way, t), v], dst_ref=piece(chip_of(way, t) * 2 + core, p),
-            send_sem=hs.at[way, t, v], recv_sem=hr.at[way, t, p],
-            device_id=(owner, me), device_id_type=MESH)
+            src_ref=stage.at[chip, v], dst_ref=piece(chip * 2 + core, p),
+            send_sem=hs.at[kind, way, t, v], recv_sem=hr.at[way, t, p],
+            device_id=(owner, peer), device_id_type=MESH)
+
+    def relay_on(way, chip, t, v):
+        peer = (chip + t + 1 if way == 0 else chip - t - 1) * 2 + core
+        ref = stage.at[chip, v]
+        return remote(ref, ref, ws.at[way, t, v], wr.at[way, t, v], peer)
 
     def can_send(way, t):
         return ((c - t >= 0) & (c + 1 < C)) if way == 0 else ((c + t < C) & (c >= 1))
@@ -178,41 +188,105 @@
             return carry
         lax.fori_loop(0, n, step, 0)
 
-    JOBS = ((lo0, n0, 0, True, owner0), (0, n1, n0, False, sec), (lo2, n2, n0 + n1, True, pair))
-
-    def send_own(job):
-        lo, n, base, help_, owner = JOBS[job]
-
+    JOBS = (
+        (lo0, n0, 0, owner0),
+        (lo2, n2, n0 + n1, pair),
+        (direct[0] + across[0], n3, n0 + n1 + n2, sec - 3),
+    )
+
+    def left_over(way):
+        return C - 1 - c if way == 0 else c
+
+    def spread_far(way, chip, a, v, act):
+        @pl.when(left_over(way) >= 3)
+        def _():
+            act(relay_on(way, chip, a + 1, v))
+
+    def spread_near(way, chip, a, v, p, owner, act):
+        left = left_over(way)
+
+        @pl.when(left == 2)
+        def _():
+            act(deliver(way, chip, 0, a + 1, v, p, owner))
+
+        @pl.when(left >= 1)
+        def _():
+            act(deliver(way, chip, 0, a, v, p, owner))
+
+    def spread(way, chip, a, v, p, owner, act):
+        spread_far(way, chip, a, v, act)
+        spread_near(way, chip, a, v, p, owner, act)
+
+    far_end = (left_over(0) >= 3) | (left_over(1) >= 3)
+
+    def start(copy):
+        copy.start()
+
+    def sent_out(copy):
+        copy.wait_send()
+
+    def own_sends(act):
         def one(p, i):
-            v = base + i
-            if help_:
-                enter(p, v, owner).wait_recv()
             for way in range(2):
                 @pl.when(can_send(way, 0))
                 def _(way=way):
-                    line_copy(way, 0, v, held(help_, c, v, p)).start()
+                    act(line_copy(way, 0, n0 + i, piece(c * 2 + core, p)))
+        loop(0, n1, one)
+
+    def help_far(job, act, arrive):
+        lo, n, base, owner = JOBS[job]
+
+        def one(p, i):
+            @pl.when(far_end)
+            def _():
+                if arrive:
+                    enter(p, base + i, owner).wait_recv()
+                for way in range(2):
+                    spread_far(way, c, 0, base + i, act)
         loop(lo, n, one)
 
-    def serve(job, t):
-        lo, n, base, help_, owner = JOBS[job]
+    def help_near(job, act, arrive):
+        lo, n, base, owner = JOBS[job]
 
         def one(p, i):
-            v = base + i
+            if arrive:
+                @pl.when(jnp.logical_not(far_end))
+                def _():
+                    enter(p, base + i, owner).wait_recv()
+            for way in range(2):
+                spread_near(way, c, 0, base + i, p, owner, act)
+        loop(lo, n, one)
+
+    def help_on(job, act, arrive):
+        lo, n, base, owner = JOBS[job]
+        for t in range(1, C - 1, 2):
+            def one(p, i, t=t):
+                v = base + i
+                for way in range(2):
+                    @pl.when(can_recv(way, t) & (left_over(way) >= 1))
+                    def _(way=way):
+                        chip = chip_of(way, t)
+                        if arrive:
+                            relay_on(way, chip, t, v).wait_recv()
+                        spread(way, chip, t + 1, v, p, owner, act)
+                        act(deliver(way, chip, 1, t, v, p, owner))
+            loop(lo, n, one)
+
+    def serve(t):
+        def one(p, i):
+            v = n0 + i
             for way in range(2):
                 @pl.when(can_recv(way, t))
                 def _(way=way):
                     chip = chip_of(way, t)
-                    ref = held(help_, chip, v, p)
+                    ref = piece(chip * 2 + core, p)
                     line_copy(way, t, v, ref).wait_recv()
                     if t + 1 < C - 1:
                         @pl.when(can_send(way, t + 1))
                         def _():
                             line_copy(way, t + 1, v, ref).start()
-                    if help_:
-                        hand(way, t, v, p, owner).start()
-                    else:
-                        relay(1 + way * (C - 1) + t, chip, p, True).start()
-        loop(lo, n, one)
+                    relay(1 + way * (C - 1) + t, chip, p, True).start()
+        loop(0, n1, one)
 
     def handed(t):
         def one(p, i):
@@ -233,20 +307,21 @@
         def one(p, i):
             act(enter(p, far + i, pair))
         loop(n1, by_role(across), one)
-
-        @pl.when(role == 3)
-        def _():
-            def other(p, i):
-                act(enter(p, i, sec - 1))
-            loop(direct[3] + across[3], near[3], other)
-
-    enter_all(lambda copy: copy.start())
+        for r, base, step in ((3, 0, -1), (0, direct[3] + across[1], 3)):
+            @pl.when(role == r)
+            def _(r=r, base=base, step=step):
+                def other(p, i):
+                    act(enter(p, base + i, sec + step))
+                loop(direct[r] + across[r], near[r], other)
+
+    enter_all(start)
 
     @pl.when(n0 == 0)
     def _():
-        send_own(1)
+        own_sends(start)
     remote(wall.at[me], wall.at[me], rls.at[0], rlr.at[0], partner).start()
-    send_own(0)
+    help_far(0, start, True)
+    help_near(0, start, True)
 
     def cot_copy(k, j):
         return pltpu.make_async_copy(
@@ -293,35 +368,37 @@
                 acc[...] += dot_nn(ns[chip * 2], wall[chip * 2]) + dot_nn(
                     ns[chip * 2 + 1], wall[chip * 2 + 1])
 
+    help_on(0, start, True)
+
+    @pl.when(n0 > 0)
+    def _():
+        own_sends(start)
+    relayed(0, c, False, rlr)
+    acc[...] = dot_nn(ns[c * 2], wall[c * 2]) + dot_nn(ns[c * 2 + 1], wall[c * 2 + 1])
+    for t in range(C - 1):
+        serve(t)
+        if 0 < t < C - 2:
+            handed(t - 1)
+
+    for job in (1, 2):
+        help_far(job, start, True)
+    for job in (1, 2):
+        help_near(job, start, True)
+
     def send_rows():
         for i in range(1, N):
             peer = (me + i) % N
             remote(ns.at[peer], nall.at[me], nsem.at[0], nsem.at[1], peer).start()
 
-    for t in range(C - 1):
-        serve(0, t)
-        if t == 0:
-            @pl.when(n0 > 0)
-            def _():
-                send_own(1)
-    relayed(0, c, False, rlr)
-    acc[...] = dot_nn(ns[c * 2], wall[c * 2]) + dot_nn(ns[c * 2 + 1], wall[c * 2 + 1])
-    for t in range(C - 1):
-        serve(1, t)
-        if t == 0:
-            send_own(2)
-        if t > 0:
-            handed(t - 1)
-        if t > 1:
-            use_step(t - 2)
+    @pl.when((role < 2) if shared else (role >= 0))
+    def _():
+        send_rows()
+    if C > 2:
+        handed(C - 3)
+    for t in range(C - 2):
+        use_step(t)
     handed(C - 2)
-    if C > 2:
-        use_step(C - 3)
     use_step(C - 2)
-
-    @pl.when(n2 == 0)
-    def _():
-        send_rows()
 
     row_pos = lax.broadcasted_iota(jnp.int32, (L, L), 0)
     col_pos = lax.broadcasted_iota(jnp.int32, (L, L), 1)
@@ -355,6 +432,26 @@
         ref = kball.at[me, k, j]
         return remote(ref, ref, kbs.at[k, 0], kbr.at[k, 0], partner)
 
+    def kbsends(k, j, i):
+        right = (i == 1) & (c + 1 < C)
+        left = (i == C - 1) & (c >= 1)
+        return (sec == 0) | right | left
+
+    def kbshare(k, j):
+        kbpartner(k, j).start()
+        for i in range(1, C):
+            @pl.when(kbsends(k, j, i))
+            def _(i=i):
+                kbcopy(k, j, i).start()
+
+    def from_chip(way, t):
+        return t + 1 if way == 0 else C - 1 - t
+
+    def kbpass(k, way, t):
+        ref = kball.at[chip_of(way, t) * 2 + core, k]
+        peer = (c + 1 if way == 0 else c - 1) * 2 + core
+        return remote(ref, ref, kfs.at[k, way, t], kbr.at[k, from_chip(way, t + 1)], peer)
+
     def kbrelay(k, i, mine):
         chip = (c - i + C) % C
         ref = kball.at[chip * 2 + (core if mine else 1 - core), k]
@@ -369,6 +466,11 @@
     def turn(k, carry):
         rows = pl.ds(pl.multiple_of(k * L, L), L)
         keys, values = [], []
+
+        @pl.when((k == B - 1) & (role >= 2))
+        def _():
+            for job in (1, 2):
+                help_on(job, start, True)
         for j in range(KH):
             @pl.when(sec == S - 1)
             def _(j=j):
@@ -396,9 +498,9 @@
                 col = (j * G + g) * HEAD_DIM
                 gnb[col // w, :, col % w:col % w + HEAD_DIM] = (
                     v * cos - pltpu.roll(v, HEAD_DIM // 2, 1) * sin)
-            kbpartner(k, j).start()
-            for i in range(1, C):
-                kbcopy(k, j, i).start()
+            @pl.when(sec == 0)
+            def _(j=j):
+                kbshare(k, j)
         @pl.when((sec == S - 1) & (k > 0))
         def _():
             sent(k - 1)
@@ -431,12 +533,33 @@
         return carry
     lax.fori_loop(0, B, turn, 0)
 
-    for t in range(C - 1):
-        serve(2, t)
-
-    @pl.when(n2 > 0)
-    def _():
-        send_rows()
+    for job in range(3):
+        help_far(job, sent_out, False)
+        help_near(job, sent_out, False)
+        help_on(job, sent_out, False)
+    if shared:
+        @pl.when(role >= 2)
+        def _():
+            half = C // 2
+
+            @pl.when((c >= 1) & (c < half))
+            def _():
+                pl.semaphore_signal(release, inc=1, device_id=(sec, me - 2), device_id_type=MESH)
+
+            @pl.when((c >= half) & (c < C - 1))
+            def _():
+                pl.semaphore_signal(release, inc=1, device_id=(sec, me + 2), device_id_type=MESH)
+
+            @pl.when((c < half - 1) | (c > half))
+            def _():
+                pl.semaphore_wait(release, 1)
+            send_rows()
+
+    @pl.when(sec > 0)
+    def _():
+        for k in range(B):
+            for j in range(KH):
+                kbshare(k, j)
 
     @pl.when((sec == S - 1) & (core == 0))
     def _():
@@ -448,10 +571,17 @@
         peer = (me + i) % N
         remote(gsh.at[peer], gsall.at[me], ssem.at[0], ssem.at[1], peer).start()
     for k in range(B):
-        for i in range(1, C):
-            chip = (c - i + C) % C
-            wait_all(kball.at[chip * 2 + core, k], kbr.at[k, i])
-            kbrelay(k, i, True).start()
+        for t in range(C - 1):
+            for way in range(2):
+                @pl.when(can_recv(way, t))
+                def _(k=k, t=t, way=way):
+                    i = from_chip(way, t)
+                    wait_all(kball.at[chip_of(way, t) * 2 + core, k], kbr.at[k, i])
+                    if t + 1 < C - 1:
+                        @pl.when((sec > 0) & can_send(way, t + 1))
+                        def _():
+                            kbpass(k, way, t).start()
+                    kbrelay(k, i, True).start()
     wait_all(nall.at[pl.ds(0, N - 1)], nsem.at[1])
     for k in range(B):
         wait_all(kball.at[partner, k], kbr.at[k, 0])
@@ -474,31 +604,33 @@
     wait_all(nall.at[pl.ds(0, N - 1)], nsem.at[0])
     wait_all(gsall.at[pl.ds(0, N - 1)], ssem.at[0])
     relayed(0, c, True, rls)
-    enter_all(lambda copy: copy.wait_send())
+    enter_all(sent_out)
+    own_sends(sent_out)
     for t in range(C - 1):
-        for job in range(3):
-            lo, n, base, help_, owner = JOBS[job]
-
-            def done(p, i, t=t, base=base, help_=help_, owner=owner):
-                v = base + i
-                for way in range(2):
-                    @pl.when(can_send(way, t))
-                    def _(way=way):
-                        line_copy(way, t, v, held(help_, c, v, p)).wait_send()
-                    if help_:
-                        @pl.when(can_recv(way, t))
-                        def _(way=way):
-                            hand(way, t, v, p, owner).wait_send()
-            loop(lo, n, done)
+        def passed(p, i, t=t):
+            for way in range(2):
+                @pl.when(can_recv(way, t) & can_send(way, t + 1))
+                def _(way=way):
+                    ref = piece(chip_of(way, t) * 2 + core, p)
+                    line_copy(way, t + 1, n0 + i, ref).wait_send()
+        if t + 1 < C - 1:
+            loop(0, n1, passed)
         for way in range(2):
             @pl.when(can_recv(way, t))
             def _(way=way, t=t):
                 relayed(1 + way * (C - 1) + t, chip_of(way, t), True, rls)
     for k in range(B):
         for i in range(C):
-            wait_all(kball.at[me, k], kbs.at[k, i])
+            @pl.when(kbsends(k, 0, i) | (i == 0))
+            def _(k=k, i=i):
+                wait_all(kball.at[me, k], kbs.at[k, i])
             if i:
                 kbrelay(k, i, True).wait_send()
+        for t in range(C - 2):
+            for way in range(2):
+                @pl.when((sec > 0) & can_recv(way, t) & can_send(way, t + 1))
+                def _(k=k, t=t, way=way):
+                    kbpass(k, way, t).wait_send()
 
     @pl.when(sec < S - 1)
     def _():
@@ -517,7 +649,8 @@
     CW = D // KH
     G = CW // HEAD_DIM
     C = N // 2
-    slots = line_slots(S)
+    slots = line_slots(S, w)
+    units = shares(S, w)[0]
     cos, sin = rope_tables(L)
     gain8 = jnp.broadcast_to(norm_gain.astype(F32), (8, w))
     vmem = pl.BlockSpec(memory_space=pltpu.VMEM)
@@ -550,14 +683,15 @@
             pltpu.VMEM((N, B, KH, L, 2 * HEAD_DIM), BF16),
             pltpu.VMEM((N, 8, w), F32),
             pltpu.VMEM((N, 8, w), F32),
-            pltpu.VMEM((C, slots, w // UNITS, 2 * KV), BF16),
+            pltpu.VMEM((C, slots, w // units, 2 * KV), BF16),
             dma((2,)),
             dma((2, C - 1, slots)),
             dma((2, C - 1, slots)),
-            dma((2, C - 1, slots)),
-            dma((2, C - 1, UNITS)),
-            dma((UNITS,)),
+            dma((2, 2, C - 1, slots)),
+            dma((2, C - 1, units)),
+            dma((units,)),
             dma((slots,)),
+            pltpu.SemaphoreType.REGULAR,
             pltpu.SemaphoreType.REGULAR,
             dma((2 * C - 1,)),
             dma((2 * C - 1,)),
@@ -571,6 +705,7 @@
             dma((B, C)),
             dma((B, C)),
             dma((B, C)),
+            dma((B, 2, max(C - 2, 1))),
         ],
         compiler_params=pltpu.CompilerParams(
             collective_id=0, has_side_effects=True, vmem_limit_bytes=56 * 1024 * 1024),

time: 191 us -> 155 us (0.81); the launches traced: 188 us -> 154 us
  Pallas kernels: 178 us -> 145 us
    pallas_call x1, Pallas kernels: 178 us -> 145 us  [body(): pl.pallas_call(functools.partial(kernel, S, N), out_shape=(jax.ShapeDtype...]
where the time goes in v2:
time: 155 us; the launch traced here: 154 us
  Pallas kernels  145 us (94%)
  other arithmetic  4.5 us (3%)
  local copies, waits for them, and re-layouts  4.48 us (3%)
    pallas_call x1, Pallas kernels, body(): pl.pallas_call(functools.partial(kernel, S, N), out_shape=(jax.ShapeDtype...  145 us

profile of v2, /device:TPU:0, one launch (start us, length us, event | category | flops | bytes accessed | tf_op | source)
XLA Modules:
  0.0 154.3 jit_solution(15374547804816781757)
XLA Ops:
  0.6 0.7 iota_compare_fusion
  1.4 0.7 broadcast_in_dim.53
  2.0 0.6 broadcast_in_dim.46.gain_ref
  2.7 144.7 %shard_map.111 = (bf16[128,4096]{1,0:T(8,128)(2,1)}, f32[512,512]{1,0:T(8,128)}, f32[512,512]{1,0:T(8,128)}, f32[8,512]{1,0:T(8,128)}) custom-call(bf16[128,4096]{1,0:T(8,128)(2,1)} %bitcast.9, bf16[2,64,4096]{2,1,0:T(8,128)(2,1)} %cot_ref.1, f32[8,512]{1,0:T(8,128)} %broadcast_in_dim.46.gain_ref, bf16[512,512]{1,0:T(8,128)(2,1)} %bitcast.14, ...), custom_call_target="tpu_custom_call" | custom-call | tf_op jit(solution)/shard_map/pallas_call | solution.py:659
  147.3 0.0 copy-start.1
  147.3 3.1 %select_reduce_fusion = bf16[2,64,4096]{2,1,0:T(8,128)(2,1)} fusion(pred[2,2]{1,0:T(4,128)(4,1)S(1)} %iota_compare_fusion, bf16[2,64,4096]{2,1,0:T(8,128)(2,1)} %bitcast.11), kind=kLoop, calls=%fused_computation | loop fusion | flops 1572864 | bytes 2097156 | tf_op jit(solution)/shard_map/reduce_sum | solution.py:716
  150.4 1.3 slice.3
  151.7 0.0 copy-done.1
  151.7 0.0 copy-start
  151.7 1.0 copy.14
  152.7 0.6 copy-done
  153.3 1.0 copy.15
Async XLA Ops:
  147.3 4.4 %copy-start.1 = (f32[512,512]{1,0:T(8,128)S(1)}, f32[512,512]{1,0:T(8,128)}, u32[]{:S(2)}) copy-start(f32[512,512]{1,0:T(8,128)} %get-tuple-element.9) | copy-start | bytes 3145732
  151.7 1.6 %copy-start = (f32[512,512]{1,0:T(8,128)S(1)}, f32[512,512]{1,0:T(8,128)}, u32[]{:S(2)}) copy-start(f32[512,512]{1,0:T(8,128)} %get-tuple-element.10) | copy-start | bytes 3145732

commit v3 on v2

--- a/solution.py
+++ b/solution.py
@@ -12,8 +12,13 @@
 HEAD_DIM = 128
 EPS = 1e-05
 ROPE_BASE = 500000.0
-DIRECT = (8, 9, 7, 6)
-ACROSS = (5, 7, 9, 5)
+DIRECT = (9, 12, 8, 10)
+ACROSS = (7, 4, 8, 4)
+NS0 = 2
+NS1 = 2
+KB0 = 1
+J3T = 0
+J3H = 0
 MESH = pl.DeviceIdType.MESH
 F32 = jnp.float32
 BF16 = jnp.bfloat16
@@ -47,22 +52,22 @@
     if S % 4:
         return units, False, (units,) * 4, (0,) * 4, (0,) * 4
     direct = tuple(d * units // 16 for d in DIRECT)
-    across = tuple(a * units // 16 if r in (0, 3) else units - direct[r] for r, a in enumerate(ACROSS))
+    across = tuple(a * units // 16 if r % 3 == 0 else units - direct[r] for r, a in enumerate(ACROSS))
     return units, True, direct, across, tuple(units - d - a for d, a in zip(direct, across))
 
 
 def line_slots(S, w):
     units, shared, direct, across, near = shares(S, w)
     before = (across[2], across[3], near[3], 0)
-    after = (0, 0, across[0], across[1] + near[0])
+    after = (0, near[0], across[0], across[1])
     return max(before[r] + direct[r] + after[r] for r in range(4))
 
 
-def kernel(S, N, x_ref, cot_ref, gain_ref, wk_ref, wv_ref, cos_ref, sin_ref,
-           low_out, gk_out, gv_out, gg_out,
-           wall, ns, nall, gall, inv_s, acc, key_s, val_s, qst, prob, ubuf, lowb, gnb,
+def kernel(S, N, x_hbm, cot_ref, gain_hbm, wk_ref, wv_ref, cos_hbm, sin_hbm,
+           low_out, rows_out, back_out, gg_out,
+           x_ref, gain_ref, cos_ref, sin_ref, wall, ns, nall, gall, inv_s, acc, key_s, val_s, qst, prob, ubuf, lowb, gnb,
            kball, gsh, gsall, stage,
-           loc, ws, wr, hs, hr, es, er, token, release, rls, rlr, gsem, nsem, ssem, us, ur, uloc, kbs, kbr, krs, krr, kfs):
+           loc, ws, wr, hs, hr, es, er, token, release, rls, rlr, gsem, nsem, ssem, us, ur, uloc, kbs, kbr, krs, krr, kfs, lsem, osem):
     B, KH, L = ubuf.shape[0], ubuf.shape[1], ubuf.shape[2]
     CW = ubuf.shape[3]
     w = wall.shape[1]
@@ -90,13 +95,14 @@
     pair = jnp.where(up, sec - 2, sec + 2) if shared else sec
     first = (direct[2], direct[3], direct[3] + across[3], 0)
     counts = (across[2], across[3], near[3], 0)
-    last = (0, 0, direct[0], direct[1])
-    after = (0, 0, across[0], across[1])
     lo0, n0 = by_role(first), by_role(counts)
     n1 = by_role(direct)
-    lo2, n2 = by_role(last), by_role(after)
+    n2 = by_role((0, 0, across[0], across[1] * J3H))
+    lo2 = by_role((0, 0, direct[0], direct[1]))
+    n3 = by_role((0, near[0], 0, across[1] * (1 - J3H)))
+    lo3 = by_role((0, direct[0] + across[0], 0, direct[1]))
+    owner3 = jnp.where(role == 1, sec - 1, pair)
     owner0 = jnp.where(role == 2, sec + 1, pair)
-    n3 = by_role((0, 0, 0, near[0]))
 
     def remote(src, dst, send, recv, peer):
         return pltpu.make_async_remote_copy(
@@ -108,8 +114,15 @@
 
     ck = pltpu.make_async_copy(wk_ref, wall.at[me, :, pl.ds(0, KV)], loc.at[0])
     cv = pltpu.make_async_copy(wv_ref, wall.at[me, :, pl.ds(KV, KV)], loc.at[1])
+    small = [
+        pltpu.make_async_copy(src, dst, loc.at[2 + i])
+        for i, (src, dst) in enumerate((
+            (gain_hbm, gain_ref), (x_hbm, x_ref), (cos_hbm, cos_ref), (sin_hbm, sin_ref)))]
+    small[0].start()
     ck.start()
     cv.start()
+    for cp in small[1:]:
+        cp.start()
 
     barrier = pltpu.get_barrier_semaphore()
     for i in range(1, N):
@@ -133,12 +146,13 @@
     above = jnp.where(sec < S - 1, 1, 0)
     pl.semaphore_wait(barrier, N - 1 + below + above + (3 * C if shared else 0))
 
+    small[0].wait()
+    gall[me] = jnp.broadcast_to(gain_ref[...].astype(F32), gall.shape[1:])
     gcopies = []
     for i in range(1, N):
-        cp = remote(gain_ref, gall.at[me], gsem.at[0], gsem.at[1], (me + i) % N)
+        cp = remote(gall.at[me], gall.at[me], gsem.at[0], gsem.at[1], (me + i) % N)
         cp.start()
         gcopies.append(cp)
-    gall[me] = gain_ref[...]
     ck.wait()
     cv.wait()
 
@@ -191,7 +205,7 @@
     JOBS = (
         (lo0, n0, 0, owner0),
         (lo2, n2, n0 + n1, pair),
-        (direct[0] + across[0], n3, n0 + n1 + n2, sec - 3),
+        (lo3, n3, n0 + n1, owner3),
     )
 
     def left_over(way):
@@ -234,34 +248,34 @@
         loop(0, n1, one)
 
     def help_far(job, act, arrive):
-        lo, n, base, owner = JOBS[job]
+        lo, n, at, owner = JOBS[job]
 
         def one(p, i):
             @pl.when(far_end)
             def _():
                 if arrive:
-                    enter(p, base + i, owner).wait_recv()
+                    enter(p, at + i, owner).wait_recv()
                 for way in range(2):
-                    spread_far(way, c, 0, base + i, act)
+                    spread_far(way, c, 0, at + i, act)
         loop(lo, n, one)
 
     def help_near(job, act, arrive):
-        lo, n, base, owner = JOBS[job]
+        lo, n, at, owner = JOBS[job]
 
         def one(p, i):
             if arrive:
                 @pl.when(jnp.logical_not(far_end))
                 def _():
-                    enter(p, base + i, owner).wait_recv()
+                    enter(p, at + i, owner).wait_recv()
             for way in range(2):
-                spread_near(way, c, 0, base + i, p, owner, act)
+                spread_near(way, c, 0, at + i, p, owner, act)
         loop(lo, n, one)
 
     def help_on(job, act, arrive):
-        lo, n, base, owner = JOBS[job]
+        lo, n, at, owner = JOBS[job]
         for t in range(1, C - 1, 2):
             def one(p, i, t=t):
-                v = base + i
+                v = at + i
                 for way in range(2):
                     @pl.when(can_recv(way, t) & (left_over(way) >= 1))
                     def _(way=way):
@@ -271,6 +285,19 @@
                         spread(way, chip, t + 1, v, p, owner, act)
                         act(deliver(way, chip, 1, t, v, p, owner))
             loop(lo, n, one)
+
+    def help_direct(job, act, arrive):
+        lo, n, at, owner = JOBS[job]
+
+        def one(p, i):
+            if arrive:
+                enter(p, at + i, owner).wait_recv()
+            for way in range(2):
+                for t in reversed(range(C - 1)):
+                    @pl.when(left_over(way) > t)
+                    def _(way=way, t=t):
+                        act(deliver(way, c, 0, t, at + i, p, owner))
+        loop(lo, n, one)
 
     def serve(t):
         def one(p, i):
@@ -307,11 +334,11 @@
         def one(p, i):
             act(enter(p, far + i, pair))
         loop(n1, by_role(across), one)
-        for r, base, step in ((3, 0, -1), (0, direct[3] + across[1], 3)):
+        for r, at, step in ((3, 0, -1), (0, across[3] + direct[1], 1)):
             @pl.when(role == r)
-            def _(r=r, base=base, step=step):
+            def _(r=r, at=at, step=step):
                 def other(p, i):
-                    act(enter(p, base + i, sec + step))
+                    act(enter(p, at + i, sec + step))
                 loop(direct[r] + across[r], near[r], other)
 
     enter_all(start)
@@ -333,6 +360,8 @@
             for j in range(KH):
                 cot_copy(k, j).start()
 
+    for cp in small[1:]:
+        cp.wait()
     total = jnp.zeros((B * L, 1), F32)
     for d in range(N):
         xd = x_ref[:, d * w:(d + 1) * w].astype(F32)
@@ -370,6 +399,15 @@
 
     help_on(0, start, True)
 
+    def send_rows():
+        for i in range(1, N):
+            peer = (me + i) % N
+            remote(ns.at[peer], nall.at[me], nsem.at[0], nsem.at[1], peer).start()
+
+    @pl.when((role == 0) & (n0 > 0) & (NS0 == 0))
+    def _():
+        send_rows()
+
     @pl.when(n0 > 0)
     def _():
         own_sends(start)
@@ -377,22 +415,20 @@
     acc[...] = dot_nn(ns[c * 2], wall[c * 2]) + dot_nn(ns[c * 2 + 1], wall[c * 2 + 1])
     for t in range(C - 1):
         serve(t)
+        if t == max(C - 3, 0):
+            help_far(1, start, True)
         if 0 < t < C - 2:
             handed(t - 1)
-
-    for job in (1, 2):
-        help_far(job, start, True)
-    for job in (1, 2):
-        help_near(job, start, True)
-
-    def send_rows():
-        for i in range(1, N):
-            peer = (me + i) % N
-            remote(ns.at[peer], nall.at[me], nsem.at[0], nsem.at[1], peer).start()
-
-    @pl.when((role < 2) if shared else (role >= 0))
+    help_near(1, start, True)
+
+    @pl.when((role < 3) | (J3T == 0))
+    def _():
+        help_direct(2, start, True)
+
+    @pl.when(((role == 0) & (NS0 == 2)) | ((role == 1) & (NS1 == 2)))
     def _():
         send_rows()
+
     if C > 2:
         handed(C - 3)
     for t in range(C - 2):
@@ -418,6 +454,27 @@
         return carry
     lax.fori_loop(0, B, attend, 0)
 
+    half = C // 2
+
+    def in_turn(outward):
+        first = jnp.where(c < half, half - 1 if outward else 0, half if outward else C - 1)
+        last = jnp.where(c < half, 0 if outward else half - 1, C - 1 if outward else half)
+        away = jnp.where((c < half) == outward, -2, 2)
+
+        @pl.when(c != first)
+        def _():
+            pl.semaphore_wait(release, 1)
+
+        @pl.when(c != last)
+        def _():
+            pl.semaphore_signal(
+                release, inc=1, device_id=(sec, me + away), device_id_type=MESH)
+
+    @pl.when(((role == 1) & (NS1 == 0)) | ((role == 0) & (NS0 == 1)))
+    def _():
+        in_turn(False)
+        send_rows()
+
     def usend(k, j):
         return pltpu.make_async_remote_copy(
             src_ref=lowb.at[k, j], dst_ref=ubuf.at[k, j], send_sem=us.at[k, j],
@@ -435,7 +492,7 @@
     def kbsends(k, j, i):
         right = (i == 1) & (c + 1 < C)
         left = (i == C - 1) & (c >= 1)
-        return (sec == 0) | right | left
+        return ((sec == 0) & (KB0 == 1)) | right | left
 
     def kbshare(k, j):
         kbpartner(k, j).start()
@@ -463,14 +520,23 @@
             for j in range(KH):
                 usend(k, j).wait_send()
 
+    def low_copy(k, j):
+        rows = pl.ds(pl.multiple_of(k * L, L), L)
+        return pltpu.make_async_copy(
+            lowb.at[k, j], low_out.at[rows, pl.ds(j * CW, CW)], lsem.at[k, j])
+
     def turn(k, carry):
         rows = pl.ds(pl.multiple_of(k * L, L), L)
         keys, values = [], []
+        along = jnp.zeros((L, HEAD_DIM), F32)
 
         @pl.when((k == B - 1) & (role >= 2))
         def _():
-            for job in (1, 2):
-                help_on(job, start, True)
+            help_on(1, start, True)
+            if J3T == 1:
+                @pl.when(role == 3)
+                def _():
+                    help_direct(2, start, True)
         for j in range(KH):
             @pl.when(sec == S - 1)
             def _(j=j):
@@ -493,8 +559,12 @@
             values.append(gv)
             kball[me, k, j] = jnp.concatenate([gk, gv], axis=1)
             gq = dot_nn(gs, key)
+            at = j * HEAD_DIM
+            along = along + gk.astype(F32) * acc[rows, at:at + HEAD_DIM]
+            along = along + gv.astype(F32) * acc[rows, KV + at:KV + at + HEAD_DIM]
             for g in range(G):
                 v = gq[g * L:(g + 1) * L]
+                along = along + v * q[g * L:(g + 1) * L].astype(F32)
                 col = (j * G + g) * HEAD_DIM
                 gnb[col // w, :, col % w:col % w + HEAD_DIM] = (
                     v * cos - pltpu.roll(v, HEAD_DIM // 2, 1) * sin)
@@ -507,25 +577,23 @@
             pl.semaphore_signal(token, inc=1, device_id=(sec, partner), device_id_type=MESH)
         kbv = jnp.concatenate(keys + values, axis=1)
         part_inv = inv_s[rows, 0:1]
-        proj = jnp.zeros((L, 1), F32)
-        for d in range(N):
-            gn = gnb[d] + dot_nt(kbv, wall[d])
-            gnb[d] = gn
-            gt = gn * x_ref[rows, d * w:(d + 1) * w].astype(F32) * part_inv
-            proj = proj + jnp.sum(gt * gall[d][0:1, :], axis=-1, keepdims=True)
-            gsh[d] += jnp.sum(gt.reshape(L // 8, 8, w), axis=0)
-        proj = proj * (1.0 / D) * part_inv * part_inv
-        @pl.when((sec == S - 1) & ((k > 0) | (core > 0)))
-        def _():
-            pl.semaphore_wait(token, 1)
+        proj = jnp.sum(along, axis=-1, keepdims=True) * (1.0 / D) * part_inv * part_inv
         for j in range(KH):
             for e in range(N // KH):
                 d = j * (N // KH) + e
+                gn = gnb[d] + dot_nt(kbv, wall[d])
+                xd = x_ref[rows, d * w:(d + 1) * w].astype(F32)
+                gt = gn * xd * part_inv
+                gsh[d] += jnp.sum(gt.reshape(L // 8, 8, w), axis=0)
                 u = ubuf[k, j, :, e * w:(e + 1) * w].astype(F32)
-                xd = x_ref[rows, d * w:(d + 1) * w].astype(F32)
-                low = (u + part_inv * gall[d][0:1, :] * gnb[d] - xd * proj).astype(BF16)
+                low = (u + part_inv * gall[d][0:1, :] * gn - xd * proj).astype(BF16)
                 lowb[k, j, :, e * w:(e + 1) * w] = low
-                low_out[rows, d * w:(d + 1) * w] = low
+            if j == 0:
+                @pl.when((sec == S - 1) & ((k > 0) | (core > 0)))
+                def _():
+                    pl.semaphore_wait(token, 1)
+
+            low_copy(k, j).start()
 
             @pl.when(sec > 0)
             def _(j=j):
@@ -533,27 +601,18 @@
         return carry
     lax.fori_loop(0, B, turn, 0)
 
-    for job in range(3):
+    help_direct(2, sent_out, False)
+    for job in range(2):
         help_far(job, sent_out, False)
         help_near(job, sent_out, False)
         help_on(job, sent_out, False)
-    if shared:
-        @pl.when(role >= 2)
-        def _():
-            half = C // 2
-
-            @pl.when((c >= 1) & (c < half))
-            def _():
-                pl.semaphore_signal(release, inc=1, device_id=(sec, me - 2), device_id_type=MESH)
-
-            @pl.when((c >= half) & (c < C - 1))
-            def _():
-                pl.semaphore_signal(release, inc=1, device_id=(sec, me + 2), device_id_type=MESH)
-
-            @pl.when((c < half - 1) | (c > half))
-            def _():
-                pl.semaphore_wait(release, 1)
-            send_rows()
+    @pl.when(role >= 2)
+    def _():
+        in_turn(True)
+
+    @pl.when((role >= 2) | ((role == 0) & (n0 == 0) & (NS0 == 0)) | ((role == 1) & (NS1 == 1)))
+    def _():
+        send_rows()
 
     @pl.when(sec > 0)
     def _():
@@ -561,48 +620,6 @@
             for j in range(KH):
                 kbshare(k, j)
 
-    @pl.when((sec == S - 1) & (core == 0))
-    def _():
-        sent(B - 1)
-        pl.semaphore_signal(token, inc=1, device_id=(sec, partner), device_id_type=MESH)
-
-    gsall[me] = gsh[me]
-    for i in range(1, N):
-        peer = (me + i) % N
-        remote(gsh.at[peer], gsall.at[me], ssem.at[0], ssem.at[1], peer).start()
-    for k in range(B):
-        for t in range(C - 1):
-            for way in range(2):
-                @pl.when(can_recv(way, t))
-                def _(k=k, t=t, way=way):
-                    i = from_chip(way, t)
-                    wait_all(kball.at[chip_of(way, t) * 2 + core, k], kbr.at[k, i])
-                    if t + 1 < C - 1:
-                        @pl.when((sec > 0) & can_send(way, t + 1))
-                        def _():
-                            kbpass(k, way, t).start()
-                    kbrelay(k, i, True).start()
-    wait_all(nall.at[pl.ds(0, N - 1)], nsem.at[1])
-    for k in range(B):
-        wait_all(kball.at[partner, k], kbr.at[k, 0])
-        for i in range(1, C):
-            kbrelay(k, i, False).wait_recv()
-    rows_all = nall[...].reshape(N * B * L, w)
-    for j in range(KH):
-        back = jnp.concatenate(
-            [kball[g, k, j] for g in range(N) for k in range(B)], axis=0)
-        dw = dot_tn(rows_all, back)
-        gk_out[:, j * HEAD_DIM:(j + 1) * HEAD_DIM] = dw[:, :HEAD_DIM]
-        gv_out[:, j * HEAD_DIM:(j + 1) * HEAD_DIM] = dw[:, HEAD_DIM:]
-    wait_all(gsall.at[pl.ds(0, N - 1)], ssem.at[1])
-    gg = gsall[0]
-    for d in range(1, N):
-        gg = gg + gsall[d]
-    gg_out[...] = jnp.broadcast_to(jnp.sum(gg, axis=0, keepdims=True), gg_out.shape)
-
-    wait_all(gall.at[pl.ds(0, N - 1)], gsem.at[0])
-    wait_all(nall.at[pl.ds(0, N - 1)], nsem.at[0])
-    wait_all(gsall.at[pl.ds(0, N - 1)], ssem.at[0])
     relayed(0, c, True, rls)
     enter_all(sent_out)
     own_sends(sent_out)
@@ -619,6 +636,50 @@
             @pl.when(can_recv(way, t))
             def _(way=way, t=t):
                 relayed(1 + way * (C - 1) + t, chip_of(way, t), True, rls)
+
+    @pl.when((sec == S - 1) & (core == 0))
+    def _():
+        sent(B - 1)
+        pl.semaphore_signal(token, inc=1, device_id=(sec, partner), device_id_type=MESH)
+
+    gsall[me] = gsh[me]
+    for i in range(1, N):
+        peer = (me + i) % N
+        remote(gsh.at[peer], gsall.at[me], ssem.at[0], ssem.at[1], peer).start()
+    for k in range(B):
+        for t in range(C - 1):
+            for way in range(2):
+                @pl.when(can_recv(way, t))
+                def _(k=k, t=t, way=way):
+                    i = from_chip(way, t)
+                    wait_all(kball.at[chip_of(way, t) * 2 + core, k], kbr.at[k, i])
+                    if t + 1 < C - 1:
+                        @pl.when(((sec > 0) | (KB0 == 0)) & can_send(way, t + 1))
+                        def _():
+                            kbpass(k, way, t).start()
+                    kbrelay(k, i, True).start()
+    wait_all(nall.at[pl.ds(0, N - 1)], nsem.at[1])
+    outs = [pltpu.make_async_copy(nall, rows_out, osem.at[B])]
+    outs[0].start()
+    for k in range(B):
+        wait_all(kball.at[partner, k], kbr.at[k, 0])
+        for i in range(1, C):
+            kbrelay(k, i, False).wait_recv()
+        cp = pltpu.make_async_copy(kball.at[:, k], back_out.at[:, k], osem.at[k])
+        cp.start()
+        outs.append(cp)
+    wait_all(gsall.at[pl.ds(0, N - 1)], ssem.at[1])
+    gg = gsall[0]
+    for d in range(1, N):
+        gg = gg + gsall[d]
+    gg_out[...] = jnp.sum(gg, axis=0, keepdims=True)
+    for k in range(B):
+        for j in range(KH):
+            low_copy(k, j).wait()
+
+    wait_all(gall.at[pl.ds(0, N - 1)], gsem.at[0])
+    wait_all(nall.at[pl.ds(0, N - 1)], nsem.at[0])
+    wait_all(gsall.at[pl.ds(0, N - 1)], ssem.at[0])
     for k in range(B):
         for i in range(C):
             @pl.when(kbsends(k, 0, i) | (i == 0))
@@ -628,7 +689,7 @@
                 kbrelay(k, i, True).wait_send()
         for t in range(C - 2):
             for way in range(2):
-                @pl.when((sec > 0) & can_recv(way, t) & can_send(way, t + 1))
+                @pl.when(((sec > 0) | (KB0 == 0)) & can_recv(way, t) & can_send(way, t + 1))
                 def _(k=k, t=t, way=way):
                     kbpass(k, way, t).wait_send()
 
@@ -640,6 +701,46 @@
     @pl.when((sec == S - 1) & (core == 1))
     def _():
         sent(B - 1)
+    for cp in outs:
+        cp.wait()
+
+
+def finish(plan_ref, low_ref, rows_ref, back_ref, gg_ref, low_out, gk_out, gv_out, gg_out,
+           low_s, rows_s, back_s, held, lsem, isem, gsem):
+    N, B, KH, L = back_ref.shape[:4]
+    w = rows_ref.shape[2]
+    fetch_rows = pltpu.make_async_copy(rows_ref, rows_s, isem.at[KH])
+    fetch_back = [
+        pltpu.make_async_copy(back_ref.at[:, :, j], back_s.at[:, :, j], isem.at[j])
+        for j in range(KH)]
+    fetch_low = [
+        pltpu.make_async_copy(
+            low_ref.at[pl.ds(pl.multiple_of(plan_ref[0, k] * L, L), L)], low_s.at[k], lsem.at[0, k])
+        for k in range(B)]
+    fetch_rows.start()
+    for cp in fetch_back + fetch_low:
+        cp.start()
+    gg_out[...] = gg_ref[...]
+    fetch_rows.wait()
+    rows_all = rows_s[...].reshape(N * B * L, w)
+    copies = []
+    for j in range(KH):
+        fetch_back[j].wait()
+        back = jnp.concatenate(
+            [back_s[g, k, j] for g in range(N) for k in range(B)], axis=0)
+        dw = dot_tn(rows_all, back)
+        for i, out in enumerate((gk_out, gv_out)):
+            held[i, j] = dw[:, i * HEAD_DIM:(i + 1) * HEAD_DIM]
+            copies.append(pltpu.make_async_copy(
+                held.at[i, j], out.at[0, :, pl.ds(j * HEAD_DIM, HEAD_DIM)], gsem.at[i, j]))
+            copies[-1].start()
+        if j == 0:
+            for k in range(B):
+                fetch_low[k].wait()
+                copies.append(pltpu.make_async_copy(low_s.at[k], low_out.at[0, k], lsem.at[1, k]))
+                copies[-1].start()
+    for cp in copies:
+        cp.wait()
 
 
 def body(S, N, inputs, cotangent, norm_gain, key_weight, value_weight, plan):
@@ -652,21 +753,24 @@
     slots = line_slots(S, w)
     units = shares(S, w)[0]
     cos, sin = rope_tables(L)
-    gain8 = jnp.broadcast_to(norm_gain.astype(F32), (8, w))
     vmem = pl.BlockSpec(memory_space=pltpu.VMEM)
     hbm = pl.BlockSpec(memory_space=pl.ANY)
     dma = pltpu.SemaphoreType.DMA
-    low, gk, gv, gg = pl.pallas_call(
+    low, rows, back, gg = pl.pallas_call(
         functools.partial(kernel, S, N),
         out_shape=(
             jax.ShapeDtypeStruct((B * L, D), BF16),
-            jax.ShapeDtypeStruct((w, KV), F32),
-            jax.ShapeDtypeStruct((w, KV), F32),
-            jax.ShapeDtypeStruct((8, w), F32),
+            jax.ShapeDtypeStruct((N, B * L, w), BF16),
+            jax.ShapeDtypeStruct((N, B, KH, L, 2 * HEAD_DIM), BF16),
+            jax.ShapeDtypeStruct((1, w), F32),
         ),
-        in_specs=[vmem, hbm, vmem, hbm, hbm, vmem, vmem],
-        out_specs=(vmem,) * 4,
+        in_specs=[hbm] * 7,
+        out_specs=(hbm, hbm, hbm, vmem),
         scratch_shapes=[
+            pltpu.VMEM((B * L, D), BF16),
+            pltpu.VMEM((1, w), BF16),
+            pltpu.VMEM((L, HEAD_DIM), F32),
+            pltpu.VMEM((L, HEAD_DIM), F32),
             pltpu.VMEM((N, w, 2 * KV), BF16),
             pltpu.VMEM((N, B * L, w), BF16),
             pltpu.VMEM((N, B * L, w), BF16),
@@ -684,7 +788,7 @@
             pltpu.VMEM((N, 8, w), F32),
             pltpu.VMEM((N, 8, w), F32),
             pltpu.VMEM((C, slots, w // units, 2 * KV), BF16),
-            dma((2,)),
+            dma((6,)),
             dma((2, C - 1, slots)),
             dma((2, C - 1, slots)),
             dma((2, 2, C - 1, slots)),
@@ -706,16 +810,35 @@
             dma((B, C)),
             dma((B, C)),
             dma((B, 2, max(C - 2, 1))),
+            dma((B, KH)),
+            dma((B + 1,)),
         ],
         compiler_params=pltpu.CompilerParams(
             collective_id=0, has_side_effects=True, vmem_limit_bytes=56 * 1024 * 1024),
-    )(inputs[0].reshape(B * L, D), cotangent, gain8, key_weight[0], value_weight[0],
+    )(inputs[0].reshape(B * L, D), cotangent, norm_gain, key_weight[0], value_weight[0],
       jnp.asarray(cos), jnp.asarray(sin))
-    low = low.reshape(B, L, D)
-    selector = plan[0][:, None] == jnp.arange(B, dtype=jnp.int32)[None, :]
-    ordered = jnp.sum(
-        jnp.where(selector[:, :, None, None], low[None], jnp.zeros((), BF16)), axis=1)
-    return ordered[None], gk[None], gv[None], gg[0:1]
+    ordered, gk, gv, gg = pl.pallas_call(
+        finish,
+        out_shape=(
+            jax.ShapeDtypeStruct((1, B, L, D), BF16),
+            jax.ShapeDtypeStruct((1, w, KV), F32),
+            jax.ShapeDtypeStruct((1, w, KV), F32),
+            jax.ShapeDtypeStruct((1, w), F32),
+        ),
+        in_specs=[pl.BlockSpec(memory_space=pltpu.SMEM), hbm, hbm, hbm, vmem],
+        out_specs=(hbm, hbm, hbm, vmem),
+        scratch_shapes=[
+            pltpu.VMEM((B, L, D), BF16),
+            pltpu.VMEM((N, B * L, w), BF16),
+            pltpu.VMEM((N, B, KH, L, 2 * HEAD_DIM), BF16),
+            pltpu.VMEM((2, KH, w, HEAD_DIM), F32),
+            dma((2, B)),
+            dma((KH + 1,)),
+            dma((2, KH)),
+        ],
+        compiler_params=pltpu.CompilerParams(vmem_limit_bytes=56 * 1024 * 1024),
+    )(plan, low, rows, back, gg)
+    return ordered, gk, gv, gg
 
 
 def solution(mesh):

time: 155 us -> 143 us (0.923)
  the two profiles are of different devices: /device:TPU:0 before, /device:TPU:4 now
where the time goes in v3:
time: 143 us
  Pallas kernels  142 us (99%)
    pallas_call x1, Pallas kernels, body(): pl.pallas_call(functools.partial(kernel, S, N), out_shape=(jax.ShapeDtype...  136 us
    pallas_call x1, Pallas kernels, body(): pl.pallas_call(finish, out_shape=(jax.ShapeDtypeStruct((1, B, L, D), BF16...  6.44 us

profile of v3, /device:TPU:4, one launch (start us, length us, event | category | flops | bytes accessed | tf_op | source)
XLA Modules:
  0.0 142.9 jit_solution(13104466576638263466)
XLA Ops:
  0.6 135.7 %shard_map.111 = (bf16[128,4096]{1,0:T(8,128)(2,1)}, bf16[8,128,512]{2,1,0:T(8,128)(2,1)}, bf16[8,2,4,64,256]{4,3,2,1,0:T(8,128)(2,1)}, f32[1,512]{1,0:T(1,128)}) custom-call(bf16[128,4096]{1,0:T(8,128)(2,1)} %bitcast.3, bf16[2,64,4096]{2,1,0:T(8,128)(2,1)} %cot_ref.1, bf16[1,512]{1,0:T(2,128)(2,1)} %gain_hbm.1, bf16[512,512]{1,0:T(8,128)(2,1)} %bitcast.4, ...), custom_call_target="tpu_custom_call" | custom-call | tf_op jit(solution)/shard_map/pallas_call | solution.py:759
  136.3 6.4 %shard_map.112 = (bf16[1,2,64,4096]{3,2,1,0:T(8,128)(2,1)}, f32[1,512,512]{2,1,0:T(8,128)}, f32[1,512,512]{2,1,0:T(8,128)}, f32[1,512]{1,0:T(1,128)}) custom-call(s32[1,2]{1,0:T(1,128)} %plan_ref.1, bf16[128,4096]{1,0:T(8,128)(2,1)} %get-tuple-element.8.low_ref, bf16[8,128,512]{2,1,0:T(8,128)(2,1)} %get-tuple-element.9.rows_ref, ...), custom_call_target="tpu_custom_call" | custom-call | tf_op jit(solution)/shard_map/pallas_call | solution.py:820

commit v4 on v3

--- a/solution.py
+++ b/solution.py
@@ -12,13 +12,12 @@
 HEAD_DIM = 128
 EPS = 1e-05
 ROPE_BASE = 500000.0
-DIRECT = (9, 12, 8, 10)
-ACROSS = (7, 4, 8, 4)
+DIRECT = (9, 13, 8, 10)
+ACROSS = (7, 3, 8, 4)
 NS0 = 2
 NS1 = 2
 KB0 = 1
 J3T = 0
-J3H = 0
 MESH = pl.DeviceIdType.MESH
 F32 = jnp.float32
 BF16 = jnp.bfloat16
@@ -60,14 +59,14 @@
     units, shared, direct, across, near = shares(S, w)
     before = (across[2], across[3], near[3], 0)
     after = (0, near[0], across[0], across[1])
-    return max(before[r] + direct[r] + after[r] for r in range(4))
+    return max(1, max(before[r] + after[r] for r in range(4)))
 
 
 def kernel(S, N, x_hbm, cot_ref, gain_hbm, wk_ref, wv_ref, cos_hbm, sin_hbm,
            low_out, rows_out, back_out, gg_out,
            x_ref, gain_ref, cos_ref, sin_ref, wall, ns, nall, gall, inv_s, acc, key_s, val_s, qst, prob, ubuf, lowb, gnb,
            kball, gsh, gsall, stage,
-           loc, ws, wr, hs, hr, es, er, token, release, rls, rlr, gsem, nsem, ssem, us, ur, uloc, kbs, kbr, krs, krr, kfs, lsem, osem):
+           loc, ws, wr, hs, ar, es, er, token, release, rls, rlr, gsem, nsem, ssem, us, ur, uloc, kbs, kbr, krs, krr, kfs, lsem, osem):
     B, KH, L = ubuf.shape[0], ubuf.shape[1], ubuf.shape[2]
     CW = ubuf.shape[3]
     w = wall.shape[1]
@@ -97,9 +96,8 @@
     counts = (across[2], across[3], near[3], 0)
     lo0, n0 = by_role(first), by_role(counts)
     n1 = by_role(direct)
-    n2 = by_role((0, 0, across[0], across[1] * J3H))
-    lo2 = by_role((0, 0, direct[0], direct[1]))
-    n3 = by_role((0, near[0], 0, across[1] * (1 - J3H)))
+    n2 = by_role((0, 0, across[0], 0))
+    n3 = by_role((0, near[0], 0, across[1]))
     lo3 = by_role((0, direct[0] + across[0], 0, direct[1]))
     owner3 = jnp.where(role == 1, sec - 1, pair)
     owner0 = jnp.where(role == 2, sec + 1, pair)
@@ -162,9 +160,10 @@
     def chip_of(way, t):
         return c - 1 - t if way == 0 else c + 1 + t
 
-    def line_copy(way, t, v, ref):
+    def line_copy(way, t, chip, p):
         peer = (c + 1 if way == 0 else c - 1) * 2 + core
-        return remote(ref, ref, ws.at[way, t, v], wr.at[way, t, v], peer)
+        ref = piece(chip * 2 + core, p)
+        return remote(ref, ref, ws.at[0, way, t], ar.at[chip, p], peer)
 
     def relay(slot, chip, p, mine):
         ref = piece(chip * 2 + (core if mine else 1 - core), p)
@@ -173,22 +172,22 @@
     def relayed(slot, chip, mine, sem):
         wait_all(wall.at[chip * 2 + (core if mine else 1 - core)], sem.at[slot])
 
-    def enter(p, v, helper):
+    def enter(p, v, helper, kind=0):
         return pltpu.make_async_remote_copy(
-            src_ref=piece(me, p), dst_ref=stage.at[c, v], send_sem=es.at[p],
+            src_ref=piece(me, p), dst_ref=stage.at[c, v], send_sem=es.at[kind],
             recv_sem=er.at[v], device_id=(helper, me), device_id_type=MESH)
 
-    def deliver(way, chip, kind, t, v, p, owner):
+    def deliver(job, way, chip, kind, t, v, p, owner):
         peer = (chip + t + 1 if way == 0 else chip - t - 1) * 2 + core
         return pltpu.make_async_remote_copy(
             src_ref=stage.at[chip, v], dst_ref=piece(chip * 2 + core, p),
-            send_sem=hs.at[kind, way, t, v], recv_sem=hr.at[way, t, p],
+            send_sem=hs.at[min(job, 1), kind, way, t], recv_sem=ar.at[chip, p],
             device_id=(owner, peer), device_id_type=MESH)
 
-    def relay_on(way, chip, t, v):
+    def relay_on(job, way, chip, t, v):
         peer = (chip + t + 1 if way == 0 else chip - t - 1) * 2 + core
         ref = stage.at[chip, v]
-        return remote(ref, ref, ws.at[way, t, v], wr.at[way, t, v], peer)
+        return remote(ref, ref, ws.at[1 + job, way, t], wr.at[chip, v], peer)
 
     def can_send(way, t):
         return ((c - t >= 0) & (c + 1 < C)) if way == 0 else ((c + t < C) & (c >= 1))
@@ -204,74 +203,63 @@
 
     JOBS = (
         (lo0, n0, 0, owner0),
-        (lo2, n2, n0 + n1, pair),
-        (lo3, n3, n0 + n1, owner3),
+        (direct[0], n2, n0, pair),
+        (lo3, n3, n0, owner3),
     )
 
     def left_over(way):
         return C - 1 - c if way == 0 else c
 
-    def spread_far(way, chip, a, v, act):
-        @pl.when(left_over(way) >= 3)
-        def _():
-            act(relay_on(way, chip, a + 1, v))
-
-    def spread_near(way, chip, a, v, p, owner, act):
+    def spread_far(job, way, chip, a, v):
+        if a + 1 < C - 1:
+            @pl.when(left_over(way) >= 3)
+            def _():
+                relay_on(job, way, chip, a + 1, v).start()
+
+    def spread_near(job, way, chip, a, v, p, owner):
         left = left_over(way)
-
-        @pl.when(left == 2)
-        def _():
-            act(deliver(way, chip, 0, a + 1, v, p, owner))
+        if a + 1 < C - 1:
+            @pl.when(left == 2)
+            def _():
+                deliver(job, way, chip, 0, a + 1, v, p, owner).start()
 
         @pl.when(left >= 1)
         def _():
-            act(deliver(way, chip, 0, a, v, p, owner))
-
-    def spread(way, chip, a, v, p, owner, act):
-        spread_far(way, chip, a, v, act)
-        spread_near(way, chip, a, v, p, owner, act)
+            deliver(job, way, chip, 0, a, v, p, owner).start()
 
     far_end = (left_over(0) >= 3) | (left_over(1) >= 3)
 
-    def start(copy):
-        copy.start()
-
-    def sent_out(copy):
-        copy.wait_send()
-
-    def own_sends(act):
+    def own_sends():
         def one(p, i):
             for way in range(2):
                 @pl.when(can_send(way, 0))
                 def _(way=way):
-                    act(line_copy(way, 0, n0 + i, piece(c * 2 + core, p)))
+                    line_copy(way, 0, c, p).start()
         loop(0, n1, one)
 
-    def help_far(job, act, arrive):
+    def help_far(job):
         lo, n, at, owner = JOBS[job]
 
         def one(p, i):
             @pl.when(far_end)
             def _():
-                if arrive:
-                    enter(p, at + i, owner).wait_recv()
+                enter(p, at + i, owner).wait_recv()
                 for way in range(2):
-                    spread_far(way, c, 0, at + i, act)
+                    spread_far(job, way, c, 0, at + i)
         loop(lo, n, one)
 
-    def help_near(job, act, arrive):
+    def help_near(job):
         lo, n, at, owner = JOBS[job]
 
         def one(p, i):
-            if arrive:
-                @pl.when(jnp.logical_not(far_end))
-                def _():
-                    enter(p, at + i, owner).wait_recv()
+            @pl.when(jnp.logical_not(far_end))
+            def _():
+                enter(p, at + i, owner).wait_recv()
             for way in range(2):
-                spread_near(way, c, 0, at + i, p, owner, act)
+                spread_near(job, way, c, 0, at + i, p, owner)
         loop(lo, n, one)
 
-    def help_on(job, act, arrive):
+    def help_on(job):
         lo, n, at, owner = JOBS[job]
         for t in range(1, C - 1, 2):
             def one(p, i, t=t):
@@ -280,38 +268,35 @@
                     @pl.when(can_recv(way, t) & (left_over(way) >= 1))
                     def _(way=way):
                         chip = chip_of(way, t)
-                        if arrive:
-                            relay_on(way, chip, t, v).wait_recv()
-                        spread(way, chip, t + 1, v, p, owner, act)
-                        act(deliver(way, chip, 1, t, v, p, owner))
+                        relay_on(job, way, chip, t, v).wait_recv()
+                        spread_far(job, way, chip, t + 1, v)
+                        spread_near(job, way, chip, t + 1, v, p, owner)
+                        deliver(job, way, chip, 1, t, v, p, owner).start()
             loop(lo, n, one)
 
-    def help_direct(job, act, arrive):
+    def help_direct(job):
         lo, n, at, owner = JOBS[job]
 
         def one(p, i):
-            if arrive:
-                enter(p, at + i, owner).wait_recv()
+            enter(p, at + i, owner).wait_recv()
             for way in range(2):
                 for t in reversed(range(C - 1)):
                     @pl.when(left_over(way) > t)
                     def _(way=way, t=t):
-                        act(deliver(way, c, 0, t, at + i, p, owner))
+                        deliver(job, way, c, 0, t, at + i, p, owner).start()
         loop(lo, n, one)
 
     def serve(t):
         def one(p, i):
-            v = n0 + i
             for way in range(2):
                 @pl.when(can_recv(way, t))
                 def _(way=way):
                     chip = chip_of(way, t)
-                    ref = piece(chip * 2 + core, p)
-                    line_copy(way, t, v, ref).wait_recv()
+                    line_copy(way, t, chip, p).wait_recv()
                     if t + 1 < C - 1:
                         @pl.when(can_send(way, t + 1))
                         def _():
-                            line_copy(way, t + 1, v, ref).start()
+                            line_copy(way, t + 1, chip, p).start()
                     relay(1 + way * (C - 1) + t, chip, p, True).start()
         loop(0, n1, one)
 
@@ -322,33 +307,33 @@
                 def _(way=way):
                     chip = chip_of(way, t)
                     ref = piece(chip * 2 + core, p)
-                    remote(ref, ref, hs.at[way, t, 0], hr.at[way, t, p], partner).wait_recv()
+                    remote(ref, ref, ws.at[0, way, t], ar.at[chip, p], partner).wait_recv()
                     relay(1 + way * (C - 1) + t, chip, p, True).start()
         loop(n1, UNITS - n1, one)
 
-    def enter_all(act):
+    def enter_all():
         if not shared:
             return
-        far = by_role((near[3] + direct[2], direct[3], 0, 0))
+        far = by_role((near[3], 0, 0, 0))
 
         def one(p, i):
-            act(enter(p, far + i, pair))
+            enter(p, far + i, pair).start()
         loop(n1, by_role(across), one)
-        for r, at, step in ((3, 0, -1), (0, across[3] + direct[1], 1)):
+        for r, at, step in ((3, 0, -1), (0, across[3], 1)):
             @pl.when(role == r)
             def _(r=r, at=at, step=step):
                 def other(p, i):
-                    act(enter(p, at + i, sec + step))
+                    enter(p, at + i, sec + step, 1).start()
                 loop(direct[r] + across[r], near[r], other)
 
-    enter_all(start)
+    enter_all()
 
     @pl.when(n0 == 0)
     def _():
-        own_sends(start)
+        own_sends()
     remote(wall.at[me], wall.at[me], rls.at[0], rlr.at[0], partner).start()
-    help_far(0, start, True)
-    help_near(0, start, True)
+    help_far(0)
+    help_near(0)
 
     def cot_copy(k, j):
         return pltpu.make_async_copy(
@@ -397,7 +382,7 @@
                 acc[...] += dot_nn(ns[chip * 2], wall[chip * 2]) + dot_nn(
                     ns[chip * 2 + 1], wall[chip * 2 + 1])
 
-    help_on(0, start, True)
+    help_on(0)
 
     def send_rows():
         for i in range(1, N):
@@ -410,20 +395,20 @@
 
     @pl.when(n0 > 0)
     def _():
-        own_sends(start)
+        own_sends()
     relayed(0, c, False, rlr)
     acc[...] = dot_nn(ns[c * 2], wall[c * 2]) + dot_nn(ns[c * 2 + 1], wall[c * 2 + 1])
     for t in range(C - 1):
         serve(t)
         if t == max(C - 3, 0):
-            help_far(1, start, True)
+            help_far(1)
         if 0 < t < C - 2:
             handed(t - 1)
-    help_near(1, start, True)
+    help_near(1)
 
     @pl.when((role < 3) | (J3T == 0))
     def _():
-        help_direct(2, start, True)
+        help_direct(2)
 
     @pl.when(((role == 0) & (NS0 == 2)) | ((role == 1) & (NS1 == 2)))
     def _():
@@ -532,11 +517,11 @@
 
         @pl.when((k == B - 1) & (role >= 2))
         def _():
-            help_on(1, start, True)
+            help_on(1)
             if J3T == 1:
                 @pl.when(role == 3)
                 def _():
-                    help_direct(2, start, True)
+                    help_direct(2)
         for j in range(KH):
             @pl.when(sec == S - 1)
             def _(j=j):
@@ -601,11 +586,37 @@
         return carry
     lax.fori_loop(0, B, turn, 0)
 
-    help_direct(2, sent_out, False)
-    for job in range(2):
-        help_far(job, sent_out, False)
-        help_near(job, sent_out, False)
-        help_on(job, sent_out, False)
+    def drained(sem, amounts):
+        for r in range(4):
+            if amounts[r]:
+                @pl.when(role == r)
+                def _(r=r):
+                    wait_all(wall.at[0, pl.ds(0, amounts[r] * hp)], sem)
+
+    for way in range(2):
+        left = left_over(way)
+        for t in range(C - 1):
+            @pl.when(left > t)
+            def _(way=way, t=t):
+                drained(hs.at[1, 0, way, t], (0, near[0], 0, across[1]))
+        for job, amounts in enumerate((counts, (0, 0, across[0], 0))):
+            for a in (0,) + tuple(range(2, C, 2)):
+                there = can_recv(way, a - 1) if a else left >= 0
+                if a + 1 < C - 1:
+                    @pl.when(there & (left >= 3))
+                    def _(way=way, a=a, job=job, amounts=amounts):
+                        drained(ws.at[1 + job, way, a + 1], amounts)
+
+                    @pl.when(there & (left == 2))
+                    def _(way=way, a=a, job=job, amounts=amounts):
+                        drained(hs.at[job, 0, way, a + 1], amounts)
+                if a < C - 1:
+                    @pl.when(there & (left >= 1))
+                    def _(way=way, a=a, job=job, amounts=amounts):
+                        drained(hs.at[job, 0, way, a], amounts)
+                        if a:
+                            drained(hs.at[job, 1, way, a - 1], amounts)
+
     @pl.when(role >= 2)
     def _():
         in_turn(True)
@@ -621,17 +632,14 @@
                 kbshare(k, j)
 
     relayed(0, c, True, rls)
-    enter_all(sent_out)
-    own_sends(sent_out)
+    if shared:
+        drained(es.at[0], across)
+        drained(es.at[1], (near[0], 0, 0, near[3]))
     for t in range(C - 1):
-        def passed(p, i, t=t):
-            for way in range(2):
-                @pl.when(can_recv(way, t) & can_send(way, t + 1))
-                def _(way=way):
-                    ref = piece(chip_of(way, t) * 2 + core, p)
-                    line_copy(way, t + 1, n0 + i, ref).wait_send()
-        if t + 1 < C - 1:
-            loop(0, n1, passed)
+        for way in range(2):
+            @pl.when(can_send(way, t) & (can_recv(way, t - 1) if t else True))
+            def _(way=way, t=t):
+                drained(ws.at[0, way, t], direct)
         for way in range(2):
             @pl.when(can_recv(way, t))
             def _(way=way, t=t):
@@ -724,17 +732,24 @@
     fetch_rows.wait()
     rows_all = rows_s[...].reshape(N * B * L, w)
     copies = []
-    for j in range(KH):
-        fetch_back[j].wait()
-        back = jnp.concatenate(
-            [back_s[g, k, j] for g in range(N) for k in range(B)], axis=0)
-        dw = dot_tn(rows_all, back)
+    for cp in fetch_back:
+        cp.wait()
+    back = jnp.concatenate([
+        jnp.concatenate(
+            [back_s[g, k, j, :, i * HEAD_DIM:(i + 1) * HEAD_DIM] for g in range(N) for k in range(B)],
+            axis=0)
+        for i in range(2) for j in range(KH)], axis=1)
+    KV = KH * HEAD_DIM
+    part = w // 2
+    for half in range(2):
+        dw = dot_tn(rows_all[:, half * part:(half + 1) * part], back)
         for i, out in enumerate((gk_out, gv_out)):
-            held[i, j] = dw[:, i * HEAD_DIM:(i + 1) * HEAD_DIM]
+            held[i, half * part:(half + 1) * part] = dw[:, i * KV:(i + 1) * KV]
             copies.append(pltpu.make_async_copy(
-                held.at[i, j], out.at[0, :, pl.ds(j * HEAD_DIM, HEAD_DIM)], gsem.at[i, j]))
+                held.at[i, pl.ds(half * part, part)], out.at[0, pl.ds(half * part, part)],
+                gsem.at[i, half]))
             copies[-1].start()
-        if j == 0:
+        if half == 0:
             for k in range(B):
                 fetch_low[k].wait()
                 copies.append(pltpu.make_async_copy(low_s.at[k], low_out.at[0, k], lsem.at[1, k]))
@@ -789,11 +804,11 @@
             pltpu.VMEM((N, 8, w), F32),
             pltpu.VMEM((C, slots, w // units, 2 * KV), BF16),
             dma((6,)),
-            dma((2, C - 1, slots)),
-            dma((2, C - 1, slots)),
-            dma((2, 2, C - 1, slots)),
-            dma((2, C - 1, units)),
-            dma((units,)),
+            dma((3, 2, C - 1)),
+            dma((C, slots)),
+            dma((2, 2, 2, C - 1)),
+            dma((C, units)),
+            dma((2,)),
             dma((slots,)),
             pltpu.SemaphoreType.REGULAR,
             pltpu.SemaphoreType.REGULAR,
@@ -831,10 +846,10 @@
             pltpu.VMEM((B, L, D), BF16),
             pltpu.VMEM((N, B * L, w), BF16),
             pltpu.VMEM((N, B, KH, L, 2 * HEAD_DIM), BF16),
-            pltpu.VMEM((2, KH, w, HEAD_DIM), F32),
+            pltpu.VMEM((2, w, KV), F32),
             dma((2, B)),
             dma((KH + 1,)),
-            dma((2, KH)),
+            dma((2, 2)),
         ],
         compiler_params=pltpu.CompilerParams(vmem_limit_bytes=56 * 1024 * 1024),
     )(plan, low, rows, back, gg)

time: 143 us -> 137 us (0.958)
  the two profiles are of different devices: /device:TPU:4 before, /device:TPU:0 now
where the time goes in v4:
time: 137 us
  Pallas kernels  137 us (100%)
    pallas_call x1, Pallas kernels, body(): pl.pallas_call(functools.partial(kernel, S, N), out_shape=(jax.ShapeDtype...  131 us
    pallas_call x1, Pallas kernels, body(): pl.pallas_call(finish, out_shape=(jax.ShapeDtypeStruct((1, B, L, D), BF16...  5.64 us

profile of v4, /device:TPU:0, one launch (start us, length us, event | category | flops | bytes accessed | tf_op | source)
XLA Modules:
  0.0 137.2 jit_solution(14914892245769556288)
XLA Ops:
  0.6 130.9 %shard_map.111 = (bf16[128,4096]{1,0:T(8,128)(2,1)}, bf16[8,128,512]{2,1,0:T(8,128)(2,1)}, bf16[8,2,4,64,256]{4,3,2,1,0:T(8,128)(2,1)}, f32[1,512]{1,0:T(1,128)}) custom-call(bf16[128,4096]{1,0:T(8,128)(2,1)} %bitcast.3, bf16[2,64,4096]{2,1,0:T(8,128)(2,1)} %cot_ref.1, bf16[1,512]{1,0:T(2,128)(2,1)} %gain_hbm.1, bf16[512,512]{1,0:T(8,128)(2,1)} %bitcast.4, ...), custom_call_target="tpu_custom_call" | custom-call | tf_op jit(solution)/shard_map/pallas_call | solution.py:774
  131.6 5.6 %shard_map.112 = (bf16[1,2,64,4096]{3,2,1,0:T(8,128)(2,1)}, f32[1,512,512]{2,1,0:T(8,128)}, f32[1,512,512]{2,1,0:T(8,128)}, f32[1,512]{1,0:T(1,128)}) custom-call(s32[1,2]{1,0:T(1,128)} %plan_ref.1, bf16[128,4096]{1,0:T(8,128)(2,1)} %get-tuple-element.8.low_ref, bf16[8,128,512]{2,1,0:T(8,128)(2,1)} %get-tuple-element.9.rows_ref, ...), custom_call_target="tpu_custom_call" | custom-call | tf_op jit(solution)/shard_map/pallas_call | solution.py:835

commit v5 on v4

--- a/solution.py
+++ b/solution.py
@@ -65,7 +65,7 @@
 def kernel(S, N, x_hbm, cot_ref, gain_hbm, wk_ref, wv_ref, cos_hbm, sin_hbm,
            low_out, rows_out, back_out, gg_out,
            x_ref, gain_ref, cos_ref, sin_ref, wall, ns, nall, gall, inv_s, acc, key_s, val_s, qst, prob, ubuf, lowb, gnb,
-           kball, gsh, gsall, stage,
+           kball, gsh, gsum, gsall, stage,
            loc, ws, wr, hs, ar, es, er, token, release, rls, rlr, gsem, nsem, ssem, us, ur, uloc, kbs, kbr, krs, krr, kfs, lsem, osem):
     B, KH, L = ubuf.shape[0], ubuf.shape[1], ubuf.shape[2]
     CW = ubuf.shape[3]
@@ -650,10 +650,12 @@
         sent(B - 1)
         pl.semaphore_signal(token, inc=1, device_id=(sec, partner), device_id_type=MESH)
 
-    gsall[me] = gsh[me]
+    for d in range(N):
+        gsum[d] = jnp.sum(gsh[d], axis=0, keepdims=True)
+    gsall[me] = gsum[me]
     for i in range(1, N):
         peer = (me + i) % N
-        remote(gsh.at[peer], gsall.at[me], ssem.at[0], ssem.at[1], peer).start()
+        remote(gsum.at[peer], gsall.at[me], ssem.at[0], ssem.at[1], peer).start()
     for k in range(B):
         for t in range(C - 1):
             for way in range(2):
@@ -680,7 +682,7 @@
     gg = gsall[0]
     for d in range(1, N):
         gg = gg + gsall[d]
-    gg_out[...] = jnp.sum(gg, axis=0, keepdims=True)
+    gg_out[...] = gg
     for k in range(B):
         for j in range(KH):
             low_copy(k, j).wait()
@@ -726,7 +728,7 @@
             low_ref.at[pl.ds(pl.multiple_of(plan_ref[0, k] * L, L), L)], low_s.at[k], lsem.at[0, k])
         for k in range(B)]
     fetch_rows.start()
-    for cp in fetch_back + fetch_low:
+    for cp in fetch_back:
         cp.start()
     gg_out[...] = gg_ref[...]
     fetch_rows.wait()
@@ -734,6 +736,8 @@
     copies = []
     for cp in fetch_back:
         cp.wait()
+    for cp in fetch_low:
+        cp.start()
     back = jnp.concatenate([
         jnp.concatenate(
             [back_s[g, k, j, :, i * HEAD_DIM:(i + 1) * HEAD_DIM] for g in range(N) for k in range(B)],
@@ -801,7 +805,8 @@
             pltpu.VMEM((N, L, w), F32),
             pltpu.VMEM((N, B, KH, L, 2 * HEAD_DIM), BF16),
             pltpu.VMEM((N, 8, w), F32),
-            pltpu.VMEM((N, 8, w), F32),
+            pltpu.VMEM((N, 1, w), F32),
+            pltpu.VMEM((N, 1, w), F32),
             pltpu.VMEM((C, slots, w // units, 2 * KV), BF16),
             dma((6,)),
             dma((3, 2, C - 1)),

time: 137 us -> 138 us (level)
  no operation moved by 1% of the time
where the time goes in v5:
time: 138 us; the launch traced here: 137 us
  Pallas kernels  137 us (99%)
    pallas_call x1, Pallas kernels, body(): pl.pallas_call(functools.partial(kernel, S, N), out_shape=(jax.ShapeDtype...  131 us
    pallas_call x1, Pallas kernels, body(): pl.pallas_call(finish, out_shape=(jax.ShapeDtypeStruct((1, B, L, D), BF16...  5.94 us

profile of v5, /device:TPU:0, one launch (start us, length us, event | category | flops | bytes accessed | tf_op | source)
XLA Modules:
  0.0 137.4 jit_solution(16292597143452652084)
XLA Ops:
  0.6 130.8 %shard_map.111 = (bf16[128,4096]{1,0:T(8,128)(2,1)}, bf16[8,128,512]{2,1,0:T(8,128)(2,1)}, bf16[8,2,4,64,256]{4,3,2,1,0:T(8,128)(2,1)}, f32[1,512]{1,0:T(1,128)}) custom-call(bf16[128,4096]{1,0:T(8,128)(2,1)} %bitcast.3, bf16[2,64,4096]{2,1,0:T(8,128)(2,1)} %cot_ref.1, bf16[1,512]{1,0:T(2,128)(2,1)} %gain_hbm.1, bf16[512,512]{1,0:T(8,128)(2,1)} %bitcast.4, ...), custom_call_target="tpu_custom_call" | custom-call | tf_op jit(solution)/shard_map/pallas_call | solution.py:778
  131.4 5.9 %shard_map.112 = (bf16[1,2,64,4096]{3,2,1,0:T(8,128)(2,1)}, f32[1,512,512]{2,1,0:T(8,128)}, f32[1,512,512]{2,1,0:T(8,128)}, f32[1,512]{1,0:T(1,128)}) custom-call(s32[1,2]{1,0:T(1,128)} %plan_ref.1, bf16[128,4096]{1,0:T(8,128)(2,1)} %get-tuple-element.8.low_ref, bf16[8,128,512]{2,1,0:T(8,128)(2,1)} %get-tuple-element.9.rows_ref, ...), custom_call_target="tpu_custom_call" | custom-call | tf_op jit(solution)/shard_map/pallas_call | solution.py:840
